TPU v7x, 16 devices: a whole 2x2x2 slice. The times are simulated.
16 devices in a mesh: ey: 2 (over z), ex: 8 (over y, x, core).
Axes of the slice: x: 2, y: 2, z: 2, core: 2. Of those that a mesh axis runs over, the one named last changes fastest.
Arguments:
- x: bfloat16 [512, 2048], P(('ey', 'ex'))
- kv_k: bfloat16 [512, 256, 4, 128], P(('ey', 'ex'))
- kv_v: bfloat16 [512, 256, 4, 128], P(('ey', 'ex'))
- lens: int32 [512], P(('ey', 'ex'))
- topk_idx: int32 [512, 4], P(('ey', 'ex'))
- gates: float32 [512, 4], P(('ey', 'ex'))
- ln1: bfloat16 [2048], replicated
- wq: bfloat16 [2048, 4096], replicated
- wo: bfloat16 [4096, 2048], replicated
- ln2: bfloat16 [2048], replicated
- ws1: bfloat16 [2048, 5632], replicated
- ws3: bfloat16 [2048, 5632], replicated
- ws2: bfloat16 [5632, 2048], replicated
- w1: bfloat16 [64, 2048, 1408], P(('ey', 'ex'))
- w3: bfloat16 [64, 2048, 1408], P(('ey', 'ex'))
- w2: bfloat16 [64, 1408, 2048], P(('ey', 'ex'))
Outputs:
- output: bfloat16 [512, 2048], P(('ey', 'ex'))
All inputs are finite; a program needn't handle non-finite values.
Results may differ from a plain program's by a relative error of at most 0.0124499.
Values are sent between devices in bfloat16 or wider.
A program may use at most 1 GiB of HBM per device.

v0:
```python
import functools

import jax
import jax.numpy as jnp
from jax import lax
from jax.experimental import pallas as pl
from jax.experimental.pallas import tpu as pltpu
from jax.sharding import PartitionSpec as P

EPS = 1e-6
GRP = ("ey", "ex")
F32 = jnp.float32
BF16 = jnp.bfloat16
MESH = pl.DeviceIdType.MESH
VMEM = pl.BlockSpec(memory_space=pltpu.VMEM)
SMEM = pl.BlockSpec(memory_space=pltpu.SMEM)
HBM = pl.BlockSpec(memory_space=pltpu.HBM)
DMA = pltpu.SemaphoreType.DMA
TOP = 4
EDEV = 4


def _rms(v32, w_ref):
    r = lax.rsqrt(jnp.mean(v32 * v32, axis=-1, keepdims=True) + EPS)
    return (v32 * r * w_ref[...].astype(F32)).astype(BF16)


def _silu_mul(z1, z3):
    return (jax.nn.silu(z1) * z3).astype(BF16)


def _attn_kernel(x_ref, ln1_ref, ln2_ref, lens_ref, wq_hbm, k_hbm, v_hbm, wo_hbm, h_ref, u_ref,
                 wq_v, k_v, v_v, wo_v, qs, os, ob, q_sem, k_sem, v_sem, o_sem):
    nq, _, qn = wq_v.shape
    nk, kb = k_v.shape[0], k_v.shape[1]
    no, _, on = wo_v.shape
    b = x_ref.shape[0]
    nh = qs.shape[0] // b
    rows = k_v.shape[2]

    def q_copy(i):
        return pltpu.make_async_copy(wq_hbm.at[:, pl.ds(pl.multiple_of(i * qn, qn), qn)], wq_v.at[i], q_sem.at[i])

    def k_copy(i):
        return pltpu.make_async_copy(k_hbm.at[i], k_v.at[i], k_sem.at[i])

    def v_copy(i):
        return pltpu.make_async_copy(v_hbm.at[i], v_v.at[i], v_sem.at[i])

    def o_copy(i):
        return pltpu.make_async_copy(wo_hbm.at[:, pl.ds(pl.multiple_of(i * on, on), on)], wo_v.at[i], o_sem.at[i])

    for i in range(nq):
        q_copy(i).start()
    a = _rms(x_ref[...].astype(F32), ln1_ref)

    @pl.loop(0, nq)
    def _(i):
        k_copy(i).start()
        v_copy(i).start()
        q_copy(i).wait()
        q = jnp.dot(a, wq_v[i], preferred_element_type=F32).astype(BF16).astype(F32)
        for j in range(qn // 128):
            qs[pl.ds(i * (qn // 128) + j, b, stride=nh), :] = q[:, j * 128:(j + 1) * 128]

    kvh = 4
    row = lax.broadcasted_iota(jnp.int32, (nh, rows), 1)
    head = lax.broadcasted_iota(jnp.int32, (nh, rows), 0)
    pos = jnp.where(row % kvh == head // (nh // kvh), row // kvh, rows)

    @pl.loop(0, nk)
    def _(i):
        o_copy(i).start()
        k_copy(i).wait()
        v_copy(i).wait()
        for j in range(kb):
            s_idx = i * kb + j
            q = qs[pl.ds(pl.multiple_of(s_idx * nh, nh), nh), :].astype(BF16)
            s = lax.dot_general(q, k_v[i, j], (((1,), (1,)), ((), ())), preferred_element_type=F32) * 128 ** -0.5
            s = jnp.where(pos < lens_ref[s_idx], s, -jnp.inf)
            m = jnp.max(s, axis=-1, keepdims=True)
            p = jnp.exp(s - m)
            p = (p / jnp.sum(p, axis=-1, keepdims=True)).astype(BF16)
            os[pl.ds(pl.multiple_of(s_idx * nh, nh), nh), :] = jnp.dot(p, v_v[i, j], preferred_element_type=F32)

    for hh in range(nh):
        ob[:, hh * 128:(hh + 1) * 128] = os[pl.ds(hh, b, stride=nh), :].astype(BF16)

    for i in range(no):
        o_copy(i).wait()
        sl = slice(i * on, (i + 1) * on)
        attn = jnp.dot(ob[...], wo_v[i], preferred_element_type=F32)
        h_ref[:, sl] = (x_ref[:, sl].astype(F32) + attn).astype(BF16)
    u_ref[...] = _rms(h_ref[...].astype(F32), ln2_ref)


def _attention(x, k, v, lens, ln1, ln2, wq, wo):
    b, d = x.shape
    nqk = wq.shape[1]
    rows = k.shape[1] * k.shape[2]
    nq = nk = no = 8
    k = k.reshape(nk, b // nk, rows, 128)
    v = v.reshape(nk, b // nk, rows, 128)
    nh = nqk // 128
    return pl.pallas_call(
        _attn_kernel,
        out_shape=[jax.ShapeDtypeStruct((b, d), BF16)] * 2,
        in_specs=[VMEM, VMEM, VMEM, SMEM, HBM, HBM, HBM, HBM],
        out_specs=[VMEM, VMEM],
        scratch_shapes=[
            pltpu.VMEM((nq, d, nqk // nq), BF16),
            pltpu.VMEM((nk, b // nk, rows, 128), BF16),
            pltpu.VMEM((nk, b // nk, rows, 128), BF16),
            pltpu.VMEM((no, nqk, d // no), BF16),
            pltpu.VMEM((b * nh, 128), F32),
            pltpu.VMEM((b * nh, 128), F32),
            pltpu.VMEM((b, nqk), BF16),
            DMA((nq,)), DMA((nk,)), DMA((nk,)), DMA((no,)),
        ],
        compiler_params=pltpu.CompilerParams(vmem_limit_bytes=62 * 2 ** 20),
        name="attn",
    )(x, ln1.reshape(1, d), ln2.reshape(1, d), lens, wq, k, v, wo)


def _place():
    z = lax.axis_index("ey")
    ex = lax.axis_index("ex")
    return z, ex // 4, (ex // 2) % 2, ex % 2


def _dev(z, y, x, c):
    return (z, y * 4 + x * 2 + c)


def _flip(v, f):
    return 1 - v if f else v


def _offset(place, d):
    z, y, x = place
    return _flip(z, d // 4), _flip(y, (d // 2) % 2), _flip(x, d % 2)


def _gather_kernel(u_ref, m_ref, w1_hbm, w3_hbm, uall_hbm, mall_ref, g_ref,
                   ua, ma, w1_v, w3_v, w1_sem, w3_sem, out_sem,
                   us_send, us_recv, uf_send, uf_recv, ms_send, ms_recv, mf_send, mf_recv):
    z, y, x, c = _place()
    nw, _, wn = w1_v.shape

    def w_copy(hbm, vm, sem, i):
        return pltpu.make_async_copy(hbm.at[:, pl.ds(i * wn, wn)], vm.at[i], sem.at[i])

    for i in range(nw):
        w_copy(w1_hbm, w1_v, w1_sem, i).start()
        w_copy(w3_hbm, w3_v, w3_sem, i).start()
    barrier = pltpu.get_barrier_semaphore()
    for d in range(1, 8):
        oz, oy, ox = _offset((z, y, x), d)
        pl.semaphore_signal(barrier, inc=1, device_id=_dev(oz, oy, ox, c), device_id_type=MESH)
    pl.semaphore_signal(barrier, inc=1, device_id=_dev(z, y, x, 1 - c), device_id_type=MESH)
    pl.semaphore_wait(barrier, 8)

    me = ((z * 2 + y) * 2 + x) * 2 + c

    def sends(d):
        dev = _dev(*_offset((z, y, x), d), c) if d else _dev(z, y, x, 1 - c)
        return (pltpu.make_async_remote_copy(u_ref, ua.at[me], us_send.at[d], us_recv.at[d], device_id=dev,
                                             device_id_type=MESH),
                pltpu.make_async_remote_copy(m_ref, ma.at[me], ms_send.at[d], ms_recv.at[d], device_id=dev,
                                             device_id_type=MESH))

    def forwards(d):
        oz, oy, ox = _offset((z, y, x), d)
        src = ((oz * 2 + oy) * 2 + ox) * 2 + c
        dev = _dev(z, y, x, 1 - c)
        return (pltpu.make_async_remote_copy(ua.at[src], ua.at[src], uf_send.at[d], uf_recv.at[d], device_id=dev,
                                             device_id_type=MESH),
                pltpu.make_async_remote_copy(ma.at[src], ma.at[src], mf_send.at[d], mf_recv.at[d], device_id=dev,
                                             device_id_type=MESH))

    order = (7, 6, 5, 3, 4, 2, 1, 0)
    for d in order:
        for cp in sends(d):
            cp.start()
    ua[me] = u_ref[...]
    ma[me] = m_ref[...]

    fwd = list(order[:-1])
    for i in range(nw):
        w_copy(w1_hbm, w1_v, w1_sem, i).wait()
        w_copy(w3_hbm, w3_v, w3_sem, i).wait()
        z1 = jnp.dot(u_ref[...], w1_v[i], preferred_element_type=F32)
        z3 = jnp.dot(u_ref[...], w3_v[i], preferred_element_type=F32)
        g_ref[:, i * wn:(i + 1) * wn] = _silu_mul(z1, z3)
        if i >= nw - 7:
            d = fwd.pop(0)
            for s, f in zip(sends(d), forwards(d)):
                s.wait_recv()
                f.start()
    for d in fwd:
        for s, f in zip(sends(d), forwards(d)):
            s.wait_recv()
            f.start()
    for cp in sends(0):
        cp.wait_recv()
    for d in range(1, 8):
        for f in forwards(d):
            f.wait_recv()
    for d in range(8):
        for s in sends(d):
            s.wait_send()
        if d:
            for f in forwards(d):
                f.wait_send()
    out = pltpu.make_async_copy(ua, uall_hbm, out_sem)
    out.start()
    mall_ref[...] = ma[...]
    out.wait()


def _gather(u, meta, ws1, ws3):
    b, d = u.shape
    fs = ws1.shape[1]
    nw = 11
    return pl.pallas_call(
        _gather_kernel,
        out_shape=[jax.ShapeDtypeStruct((16, b, d), BF16), jax.ShapeDtypeStruct((16, b, 128), F32),
                   jax.ShapeDtypeStruct((b, fs), BF16)],
        in_specs=[VMEM, VMEM, HBM, HBM],
        out_specs=[HBM, VMEM, VMEM],
        scratch_shapes=[
            pltpu.VMEM((16, b, d), BF16),
            pltpu.VMEM((16, b, 128), F32),
            pltpu.VMEM((nw, d, fs // nw), BF16),
            pltpu.VMEM((nw, d, fs // nw), BF16),
            DMA((nw,)), DMA((nw,)), DMA(()),
            DMA((8,)), DMA((8,)), DMA((8,)), DMA((8,)), DMA((8,)), DMA((8,)), DMA((8,)), DMA((8,)),
        ],
        compiler_params=pltpu.CompilerParams(vmem_limit_bytes=62 * 2 ** 20, collective_id=0, has_side_effects=True),
        name="dispatch",
    )(u, meta, ws1, ws3)


SMALL = 32
GROUP = 256


def _expert_kernel(cap, blk, u_ref, m_ref, w1_hbm, w3_hbm, w2_hbm, p_ref,
                   w1_v, w3_v, w2_v, kcol, gcol, krow, cnt, order, w_sem):
    t, d = u_ref.shape
    ng = t // GROUP
    big = cap * (GROUP // blk)
    base = (lax.axis_index("ey") * 8 + lax.axis_index("ex")) * EDEV

    lane = lax.broadcasted_iota(jnp.int32, (t, 128), 1).astype(F32) + base.astype(F32)
    hit = jnp.zeros((t, 128), F32)
    gate = jnp.zeros((t, 128), F32)
    for j in range(TOP):
        same = m_ref[:, j:j + 1] == lane
        hit += jnp.where(same, 1.0, 0.0)
        gate += jnp.where(same, m_ref[:, TOP + j:TOP + j + 1], 0.0)
    r0 = lax.broadcasted_iota(jnp.int32, (GROUP, GROUP), 0)
    r1 = lax.broadcasted_iota(jnp.int32, (GROUP, GROUP), 1)
    before = jnp.where(r1 < r0, 1.0, 0.0)
    before_blk = jnp.where(r1 // blk == r0 // blk, before, 0.0).astype(BF16)
    before = before.astype(BF16)
    for g in range(ng):
        sl = slice(g * GROUP, (g + 1) * GROUP)
        rank = jnp.dot(before_blk, hit[sl].astype(BF16), preferred_element_type=F32)
        keep = jnp.where(rank < cap, hit[sl], 0.0)
        pos = jnp.dot(before, keep.astype(BF16), preferred_element_type=F32)
        key = jnp.where(keep > 0.0, pos, -1.0)
        krow[:, sl] = key.T[0:8]
        tot = jnp.sum(keep, axis=0, keepdims=True)
        for e in range(EDEV):
            kcol[e, sl] = jnp.broadcast_to(key[:, e:e + 1], (GROUP, 128))
            gcol[e, sl] = jnp.broadcast_to(gate[sl, e:e + 1], (GROUP, 128))
            cnt[e * ng + g] = jnp.sum(tot[:, e:e + 1]).astype(jnp.int32)
    for e in range(EDEV):
        n = cnt[e * ng] + cnt[e * ng + 1]
        rank = 0
        for f in range(EDEV):
            if f != e:
                m = cnt[f * ng] + cnt[f * ng + 1]
                rank += ((m >= n) if f < e else (m > n)).astype(jnp.int32)
        order[rank] = e

    def copies(i):
        e, s = order[i], lax.rem(i, 2)
        return (pltpu.make_async_copy(w1_hbm.at[e], w1_v.at[s], w_sem.at[s, 0]),
                pltpu.make_async_copy(w3_hbm.at[e], w3_v.at[s], w_sem.at[s, 1]),
                pltpu.make_async_copy(w2_hbm.at[e], w2_v.at[s], w_sem.at[s, 2]))

    for i in range(2):
        for cp in copies(i):
            cp.start()
    p_ref[...] = jnp.zeros_like(p_ref)

    def swiglu(rows, s):
        z1 = jnp.dot(rows, w1_v[s], preferred_element_type=F32)
        z3 = jnp.dot(rows, w3_v[s], preferred_element_type=F32)
        return jnp.dot(_silu_mul(z1, z3), w2_v[s], preferred_element_type=F32).astype(BF16)

    def pick(e, g, n):
        r = lax.broadcasted_iota(jnp.int32, (n, GROUP), 0).astype(F32)
        sel = jnp.where(krow[pl.ds(e, 1), pl.ds(pl.multiple_of(g * GROUP, GROUP), GROUP)] == r, 1.0, 0.0).astype(BF16)
        rows = u_ref[pl.ds(pl.multiple_of(g * GROUP, GROUP), GROUP), :]
        return jnp.dot(sel, rows, preferred_element_type=F32).astype(BF16)

    def put(e, g, n, out):
        tl = pl.ds(pl.multiple_of(g * GROUP, GROUP), GROUP)
        r = lax.broadcasted_iota(jnp.int32, (GROUP, 128), 1).astype(F32)
        key = kcol[e, tl]
        sel = jnp.concatenate([jnp.where(key == r + 128.0 * q, 1.0, 0.0) for q in range(-(-n // 128))], axis=1)
        sel = sel[:, :n].astype(BF16)
        gt = gcol[e, tl]
        for q in range(d // 256):
            cs = slice(q * 256, (q + 1) * 256)
            back = jnp.dot(sel, out[:, cs], preferred_element_type=F32)
            p_ref[tl, cs] += back * jnp.concatenate([gt, gt], axis=1)

    @pl.loop(0, EDEV)
    def _(i):
        e, s = order[i], lax.rem(i, 2)
        for cp in copies(i):
            cp.wait()
        most = jnp.maximum(cnt[e * ng], cnt[e * ng + 1])

        @pl.when(jnp.logical_and(most > 0, most <= SMALL))
        def _():
            rows = jnp.concatenate([pick(e, g, SMALL) for g in range(ng)], axis=0)
            out = swiglu(rows, s)
            for g in range(ng):
                put(e, g, SMALL, out[g * SMALL:(g + 1) * SMALL])

        @pl.when(most > SMALL)
        def _():
            @pl.loop(0, ng)
            def _(g):
                put(e, g, big, swiglu(pick(e, g, big), s))

        @pl.when(i + 2 < EDEV)
        def _():
            for cp in copies(i + 2):
                cp.start()


def _experts(u, meta, w1, w3, w2, blk):
    t, d = u.shape
    f = w1.shape[2]
    cap = blk - blk // 8
    ng = t // GROUP
    return pl.pallas_call(
        functools.partial(_expert_kernel, cap, blk),
        out_shape=jax.ShapeDtypeStruct((t, d), F32),
        in_specs=[VMEM, VMEM, HBM, HBM, HBM],
        out_specs=VMEM,
        scratch_shapes=[
            pltpu.VMEM((2, d, f), BF16),
            pltpu.VMEM((2, d, f), BF16),
            pltpu.VMEM((2, f, d), BF16),
            pltpu.VMEM((EDEV, t, 128), F32),
            pltpu.VMEM((EDEV, t, 128), F32),
            pltpu.VMEM((8, t), F32),
            pltpu.SMEM((EDEV * ng,), jnp.int32),
            pltpu.SMEM((EDEV,), jnp.int32),
            DMA((2, 3)),
        ],
        compiler_params=pltpu.CompilerParams(vmem_limit_bytes=62 * 2 ** 20),
        name="experts",
    )(u, meta, w1, w3, w2)


COLS = ((0, 640), (640, 640), (1280, 768))


def _combine_kernel(p_hbm, g_ref, h_ref, w_hbm, y_ref,
                    acc, r0, r1, r2, r3, w_v, sh, w_sem, p_sem,
                    s0, q0, s1, q1, s2, q2, s3, q3):
    z, y, x, c = _place()
    nw, _, wn = w_v.shape

    def w_copy(i):
        return pltpu.make_async_copy(w_hbm.at[:, pl.ds(i * wn, wn)], w_v.at[i], w_sem.at[i])

    streams = [(p, half) for half in range(2) for p in range(3)]
    place = {0: x, 1: y, 2: z}

    def cols(p):
        return pl.ds(COLS[p][0], COLS[p][1])

    def rows(half):
        return pl.ds(half * 16, 16)

    def load(k):
        p, half = streams[k]
        return pltpu.make_async_copy(p_hbm.at[:, :, :, c, rows(half), cols(p)], acc.at[:, :, :, rows(half), cols(p)],
                                     p_sem.at[k])

    def swap(k):
        p, half = streams[k]
        return pltpu.make_async_remote_copy(
            p_hbm.at[:, :, :, 1 - c, rows(half), cols(p)], r0.at[:, :, :, rows(half), cols(p)], s0.at[k], q0.at[k],
            device_id=_dev(z, y, x, 1 - c), device_id_type=MESH)

    def region(ref, p, half, step, mine):
        ix = [pl.ds(0, 2)] * 3
        for s in range(step):
            dim = (p + s) % 3
            v = place[dim]
            ix[2 - dim] = v if (s < step - 1 or mine) else 1 - v
        return ref.at[ix[0], ix[1], ix[2], rows(half), cols(p)]

    def landing(p, half, step):
        ref = (r1, r2, r3)[step - 1]
        if step == 1:
            return ref.at[:, :, rows(half), cols(p)]
        if step == 2:
            return ref.at[:, rows(half), cols(p)]
        return ref.at[rows(half), cols(p)]

    def hop(k, step):
        p, half = streams[k]
        dim = (p + step - 1) % 3
        o = [z, y, x]
        o[2 - dim] = 1 - o[2 - dim]
        send, recv = ((s1, q1), (s2, q2), (s3, q3))[step - 1]
        return pltpu.make_async_remote_copy(
            region(acc, p, half, step, False), landing(p, half, step), send.at[k], recv.at[k],
            device_id=_dev(*o, c), device_id_type=MESH)

    for k in range(6):
        load(k).start()
    barrier = pltpu.get_barrier_semaphore()
    pl.semaphore_signal(barrier, inc=1, device_id=_dev(z, y, x, 1 - c), device_id_type=MESH)
    for d in (1, 2, 4):
        pl.semaphore_signal(barrier, inc=1, device_id=_dev(*_offset((z, y, x), d), c), device_id_type=MESH)
    pl.semaphore_wait(barrier, 4)
    for k in range(6):
        swap(k).start()
    for i in range(nw):
        w_copy(i).start()

    def shared(i):
        w_copy(i).wait()
        cs = slice(i * wn, (i + 1) * wn)
        sh[:, cs] = jnp.dot(g_ref[...], w_v[i], preferred_element_type=F32) + h_ref[:, cs].astype(F32)

    for k in range(6):
        p, half = streams[k]
        load(k).wait()
        swap(k).wait_recv()
        rs, cs = slice(half * 16, half * 16 + 16), slice(COLS[p][0], COLS[p][0] + COLS[p][1])
        acc[:, :, :, rs, cs] += r0[:, :, :, rs, cs]
        hop(k, 1).start()
    shared(0)
    for k in range(6):
        p, half = streams[k]
        hop(k, 1).wait_recv()
        v = region(acc, p, half, 1, True)
        v[...] += landing(p, half, 1)[...]
        hop(k, 2).start()
    shared(1)
    shared(2)
    for k in range(6):
        p, half = streams[k]
        hop(k, 2).wait_recv()
        v = region(acc, p, half, 2, True)
        v[...] += landing(p, half, 2)[...]
        hop(k, 3).start()
    for i in range(3, nw):
        shared(i)
    for k in range(6):
        p, half = streams[k]
        hop(k, 3).wait_recv()
        v = region(acc, p, half, 3, True)
        tot = v[...] + landing(p, half, 3)[...]
        rs, cs = slice(half * 16, half * 16 + 16), slice(COLS[p][0], COLS[p][0] + COLS[p][1])
        y_ref[rs, cs] = (sh[rs, cs] + tot).astype(BF16)
    for k in range(6):
        swap(k).wait_send()
        for step in (1, 2, 3):
            hop(k, step).wait_send()


def _combine(part, g, h, ws2):
    b, d = h.shape
    fs = ws2.shape[0]
    nw = 8
    part = part.reshape(2, 2, 2, 2, b, d)
    return pl.pallas_call(
        _combine_kernel,
        out_shape=jax.ShapeDtypeStruct((b, d), BF16),
        in_specs=[HBM, VMEM, VMEM, HBM],
        out_specs=VMEM,
        scratch_shapes=[
            pltpu.VMEM((2, 2, 2, b, d), F32),
            pltpu.VMEM((2, 2, 2, b, d), F32),
            pltpu.VMEM((2, 2, b, d), F32),
            pltpu.VMEM((2, b, d), F32),
            pltpu.VMEM((b, d), F32),
            pltpu.VMEM((nw, fs, d // nw), BF16),
            pltpu.VMEM((b, d), F32),
            DMA((nw,)), DMA((6,)),
            DMA((6,)), DMA((6,)), DMA((6,)), DMA((6,)), DMA((6,)), DMA((6,)), DMA((6,)), DMA((6,)),
        ],
        compiler_params=pltpu.CompilerParams(vmem_limit_bytes=62 * 2 ** 20, collective_id=1, has_side_effects=True),
        name="combine",
    )(part, g, h, ws2)


def solution(mesh):
    def body(x, kv_k, kv_v, lens, idx, gates, ln1, wq, wo, ln2, ws1, ws3, ws2, w1, w3, w2):
        b, d = x.shape
        meta = jnp.concatenate([idx.astype(F32), gates, jnp.zeros((b, 128 - 2 * TOP), F32)], axis=1)
        h, u = _attention(x, kv_k, kv_v, lens, ln1, ln2, wq, wo)
        uall, mall, g = _gather(u, meta, ws1, ws3)
        part = _experts(uall.reshape(16 * b, d), mall.reshape(16 * b, 128), w1, w3, w2, b)
        return _combine(part, g, h, ws2)

    rows = P(GRP)
    rep = P()
    return jax.shard_map(
        body, mesh=mesh,
        in_specs=(rows, rows, rows, rows, rows, rows, rep, rep, rep, rep, rep, rep, rep, rows, rows, rows),
        out_specs=rows, check_vma=False)
```

profile of v0, /device:TPU:0, one launch (start us, length us, event | category | flops | bytes accessed | tf_op | source)
XLA Modules:
  0.0 126.1 jit_solution(12573574568737445248)
XLA Ops:
  0.0 0.1 pad.2.clone
  0.1 0.7 convert_element_type.3
  0.8 1.3 %reshape.21.ln1_ref = bf16[1,2048]{1,0:T(2,128)(2,1)} reshape(bf16[2048]{0:T(1024)(128)(2,1)} %param.22) | data formatting | bytes 8192 | tf_op jit(solution)/shard_map/reshape | solution.py:122
  2.0 1.3 %reshape.22.ln2_ref = bf16[1,2048]{1,0:T(2,128)(2,1)} reshape(bf16[2048]{0:T(1024)(128)(2,1)} %param.25) | data formatting | bytes 8192 | tf_op jit(solution)/shard_map/reshape | solution.py:122
  3.3 0.1 copy.17
  3.4 0.8 copy.18
  4.2 0.7 maximum_maximum_fusion.m_ref
  4.9 28.2 %attn.1 = (bf16[32,2048]{1,0:T(8,128)(2,1)}, bf16[32,2048]{1,0:T(8,128)(2,1)}) custom-call(bf16[32,2048]{1,0:T(8,128)(2,1)} %x_ref.1, bf16[1,2048]{1,0:T(2,128)(2,1)} %reshape.21.ln1_ref, bf16[1,2048]{1,0:T(2,128)(2,1)} %reshape.22.ln2_ref, s32[32]{0:T(128)} %lens_ref.1, bf16[2048,4096]{1,0:T(8,128)(2,1)} %wq_hbm.1, bf16[8,4,1024,128]{3,2,1,0:T(8,128)(2,1)} %bitcast.6, ...), custom_call_target="tpu_custom_call" | custom-call | tf_op jit(solution)/shard_map/attn/pallas_call | solution.py:105
  33.0 27.3 %dispatch.1 = (bf16[16,32,2048]{2,1,0:T(8,128)(2,1)}, f32[16,32,128]{2,1,0:T(8,128)}, bf16[32,5632]{1,0:T(8,128)(2,1)}) custom-call(bf16[32,2048]{1,0:T(8,128)(2,1)} %get-tuple-element.10.u_ref, f32[32,128]{1,0:T(8,128)} %maximum_maximum_fusion.m_ref, bf16[2048,5632]{1,0:T(8,128)(2,1)} %w1_hbm.2, bf16[2048,5632]{1,0:T(8,128)(2,1)} %w3_hbm.2), custom_call_target="tpu_custom_call" | custom-call | tf_op jit(solution)/shard_map/dispatch/pallas_call | solution.py:225
  60.3 30.7 %experts.1 = f32[512,2048]{1,0:T(8,128)} custom-call(bf16[512,2048]{1,0:T(8,128)(2,1)} %bitcast.8, f32[512,128]{1,0:T(8,128)} %bitcast.9, bf16[4,2048,1408]{2,1,0:T(8,128)(2,1)} %w1_hbm.3, bf16[4,2048,1408]{2,1,0:T(8,128)(2,1)} %w3_hbm.3, bf16[4,1408,2048]{2,1,0:T(8,128)(2,1)} %w2_hbm.1), custom_call_target="tpu_custom_call" | custom-call | tf_op jit(solution)/shard_map/experts/pallas_call | solution.py:353
  91.0 33.6 %combine.1 = bf16[32,2048]{1,0:T(8,128)(2,1)} custom-call(f32[2,2,2,2,32,2048]{5,4,3,2,1,0:T(8,128)} %bitcast.5, bf16[32,5632]{1,0:T(8,128)(2,1)} %get-tuple-element.13.g_ref, bf16[32,2048]{1,0:T(8,128)(2,1)} %get-tuple-element.14.h_ref, bf16[5632,2048]{1,0:T(8,128)(2,1)} %w_hbm.1), custom_call_target="tpu_custom_call" | custom-call | tf_op jit(solution)/shard_map/combine/pallas_call | solution.py:491
  124.6 1.6 %copy.20 = bf16[32,2048]{1,0:T(8,128)(2,1)} copy(bf16[32,2048]{1,0:T(8,128)(2,1)} %combine.1) | data formatting | bytes 262144
  (1 shorter events, 0.0 us)
where the time goes:
time: 126 us
  Pallas kernels  120 us (95%)
  local copies, waits for them, and re-layouts  5.06 us (4%)
  other arithmetic  1.36 us (1%)
    pallas_call x1, Pallas kernels, _combine(): pl.pallas_call(_combine_kernel, out_shape=jax.ShapeDtypeStruct((b, d), BF...  33.6 us
    pallas_call x1, Pallas kernels, _experts(): pl.pallas_call(functools.partial(_expert_kernel, cap, blk), out_shape=jax...  30.7 us
    pallas_call x1, Pallas kernels, _attention(): pl.pallas_call(_attn_kernel, out_shape=[jax.ShapeDtypeStruct((b, d), BF16...  28.2 us
    pallas_call x1, Pallas kernels, _gather(): pl.pallas_call(_gather_kernel, out_shape=[jax.ShapeDtypeStruct((16, b, d)...  27.3 us

commit v1 on v0

v1 whole, which is shorter than its diff:
```python
import functools

import jax
import jax.numpy as jnp
from jax import lax
from jax.experimental import pallas as pl
from jax.experimental.pallas import tpu as pltpu
from jax.sharding import PartitionSpec as P

EPS = 1e-6
GRP = ("ey", "ex")
F32 = jnp.float32
BF16 = jnp.bfloat16
MESH = pl.DeviceIdType.MESH
VMEM = pl.BlockSpec(memory_space=pltpu.VMEM)
SMEM = pl.BlockSpec(memory_space=pltpu.SMEM)
HBM = pl.BlockSpec(memory_space=pltpu.HBM)
DMA = pltpu.SemaphoreType.DMA
TOP = 4
EDEV = 4


def _rms(v32, w):
    r = lax.rsqrt(jnp.mean(v32 * v32, axis=-1, keepdims=True) + EPS)
    return (v32 * r * w.astype(F32)).astype(BF16)


def _silu_mul(z1, z3):
    return (jax.nn.silu(z1) * z3).astype(BF16)


def _place():
    z = lax.axis_index("ey")
    ex = lax.axis_index("ex")
    return z, ex // 4, (ex // 2) % 2, ex % 2


def _dev(z, y, x, c):
    return (z, y * 4 + x * 2 + c)


def _flip(v, f):
    return 1 - v if f else v


def _offset(place, d):
    z, y, x = place
    return _flip(z, d // 4), _flip(y, (d // 2) % 2), _flip(x, d % 2)


CH = 512
RING = 18
GROUP = 256


def _front_kernel(cap, x_ref, ln1_ref, ln2_ref, idx_ref, gate_ref, lens_ref, wq_hbm, k_hbm, v_hbm, wo_hbm, ws1_hbm,
                  ws3_hbm, h_ref, uall_hbm, g_ref, key_ref, gsel_ref, krow_ref, cnt_ref,
                  ring, k_v, v_v, qs, sc, ob, us, ua, ms, ma, hit,
                  r_sem, k_sem, v_sem, out_sem, us_send, us_recv, uf_send, uf_recv, ms_send, ms_recv):
    b, d = x_ref.shape
    nqk = wq_hbm.shape[1]
    nh = nqk // 128
    nq = nqk // CH
    nk, kb, rows = k_v.shape[:3]
    nw = ws1_hbm.shape[1] // CH
    z, y, x, c = _place()
    me = ((z * 2 + y) * 2 + x) * 2 + c

    def cols(i):
        return pl.ds(i * CH if isinstance(i, int) else pl.multiple_of(i * CH, CH), CH)

    def chunk(src, n):
        s = lax.rem(n, RING)
        return pltpu.make_async_copy(src, ring.at[s], r_sem.at[s])

    def q_copy(i):
        return chunk(wq_hbm.at[:, cols(i)], i)

    def o_copy(i):
        return chunk(wo_hbm.at[pl.ds(pl.multiple_of((i % 2) * d, d), d), cols(i // 2)], nq + i)

    def w_copies(i):
        return chunk(ws1_hbm.at[:, cols(i)], 2 * nq + 2 * i), chunk(ws3_hbm.at[:, cols(i)], 2 * nq + 2 * i + 1)

    def k_copy(i):
        return pltpu.make_async_copy(k_hbm.at[i], k_v.at[i], k_sem.at[i])

    def v_copy(i):
        return pltpu.make_async_copy(v_hbm.at[i], v_v.at[i], v_sem.at[i])

    for i in range(nq):
        q_copy(i).start()
    barrier = pltpu.get_barrier_semaphore()
    peers = [_dev(*_offset((z, y, x), o % 8), _flip(c, o // 8)) for o in range(1, 16)]
    for dev in peers:
        pl.semaphore_signal(barrier, inc=1, device_id=dev, device_id_type=MESH)
    ms[...] = jnp.zeros_like(ms)
    ms[0:TOP, 0:b] = idx_ref[...].astype(F32)
    ms[TOP:2 * TOP, 0:b] = gate_ref[...]
    a = _rms(x_ref[...].astype(F32), _row(ln1_ref))

    @pl.loop(0, nq)
    def _(i):
        k_copy(i).start()
        v_copy(i).start()
        o_copy(i).start()
        q_copy(i).wait()
        q = jnp.dot(a, ring[i], preferred_element_type=F32).astype(BF16).astype(F32)
        for j in range(CH // 128):
            qs[pl.ds(i * (CH // 128) + j, b, stride=nh), :] = q[:, j * 128:(j + 1) * 128]

    pl.semaphore_wait(barrier, 15)

    def m_send(o):
        return pltpu.make_async_remote_copy(ms, ma.at[me], ms_send.at[o], ms_recv.at[o], device_id=peers[o - 1],
                                            device_id_type=MESH)

    for o in range(1, 16):
        m_send(o).start()
    ma[me] = ms[...]

    kvh = 4
    row = lax.broadcasted_iota(jnp.int32, (nh, rows), 1)
    head = lax.broadcasted_iota(jnp.int32, (nh, rows), 0)
    pos = jnp.where(row % kvh == head // (nh // kvh), row // kvh, rows)

    def of(i):
        return pl.ds(pl.multiple_of(i * nh, nh), nh)

    @pl.loop(0, nk // 2)
    def _(i):
        for cp in w_copies(i):
            cp.start()
        for t in range(2):
            k_copy(i * 2 + t).wait()
            v_copy(i * 2 + t).wait()
        seqs = [(i * 2 + t, j, (i * 2 + t) * kb + j) for t in range(2) for j in range(kb)]
        for n, (ch, j, b_i) in enumerate(seqs):
            q = qs[of(b_i), :].astype(BF16)
            s = lax.dot_general(q, k_v[ch, j], (((1,), (1,)), ((), ())), preferred_element_type=F32) * 128 ** -0.5
            sc[n] = jnp.where(pos < lens_ref[b_i], s, -jnp.inf)
        ps = []
        for n in range(len(seqs)):
            s = sc[n]
            p = jnp.exp(s - jnp.max(s, axis=-1, keepdims=True))
            ps.append((p * (1.0 / jnp.sum(p, axis=-1, keepdims=True))).astype(BF16))
        for p, (ch, j, b_i) in zip(ps, seqs):
            qs[of(b_i), :] = jnp.dot(p, v_v[ch, j], preferred_element_type=F32)

    ahead = nk // 2
    while 2 * (ahead + 1) + nq <= RING:
        for cp in w_copies(ahead):
            cp.start()
        ahead += 1

    for hh in range(nh):
        ob[:, hh * 128:(hh + 1) * 128] = qs[pl.ds(hh, b, stride=nh), :].astype(BF16)

    no = d // CH

    @pl.loop(0, no)
    def _(i):
        acc = x_ref[:, cols(i)].astype(F32)
        attn = jnp.zeros((b, CH), F32)
        for t in range(2):
            o_copy(i * 2 + t).wait()
            attn += jnp.dot(ob[:, t * d:(t + 1) * d], ring[lax.rem(nq + i * 2 + t, RING)], preferred_element_type=F32)
        h_ref[:, cols(i)] = (acc + attn).astype(BF16)
        for cp in w_copies(ahead + i):
            cp.start()

    ahead += no
    us[...] = _rms(h_ref[...].astype(F32), _row(ln2_ref))

    def shared(i):
        c1, c3 = w_copies(i)
        c1.wait()
        c3.wait()
        s = lax.rem(2 * nq + 2 * i, RING)
        z1 = jnp.dot(us[...], ring[s], preferred_element_type=F32)
        z3 = jnp.dot(us[...], ring[s + 1], preferred_element_type=F32)
        g_ref[:, cols(i)] = _silu_mul(z1, z3)

    shared(0)

    def send(o):
        dev = _dev(*_offset((z, y, x), o), c) if o else _dev(z, y, x, 1 - c)
        return pltpu.make_async_remote_copy(us, ua.at[me], us_send.at[o], us_recv.at[o], device_id=dev,
                                            device_id_type=MESH)

    def source(o, core):
        oz, oy, ox = _offset((z, y, x), o)
        return ((oz * 2 + oy) * 2 + ox) * 2 + core

    def forward(o):
        src = source(o, c)
        return pltpu.make_async_remote_copy(ua.at[src], ua.at[src], uf_send.at[o], uf_recv.at[o],
                                            device_id=_dev(z, y, x, 1 - c), device_id_type=MESH)

    def store(o, core):
        src = source(o, core)
        return pltpu.make_async_copy(ua.at[src], uall_hbm.at[src], out_sem.at[2 * o + (0 if core is c else 1)])

    order = (7, 6, 5, 3, 4, 2, 1, 0)
    for o in order:
        send(o).start()
    ua[me] = us[...]
    n = 0
    while ahead < nw:
        for cp in w_copies(ahead):
            cp.start()
        ahead += 1
        n += 1
        if ahead < nw:
            shared(n)

    for o in range(1, 16):
        m_send(o).wait_recv()
    base = ((lax.axis_index("ey") * 8 + lax.axis_index("ex")) * EDEV).astype(F32)
    turned = ma[...].reshape(128, 128).T
    lane = lax.broadcasted_iota(jnp.int32, (b, 128), 1).astype(F32) + base
    nblk = ma.shape[0]
    for i in range(nblk):
        hb = jnp.zeros((b, 128), F32)
        gb = jnp.zeros((b, 128), F32)
        for j in range(TOP):
            at = i * 2 * TOP + j
            same = turned[0:b, at:at + 1] == lane
            hb += jnp.where(same, 1.0, 0.0)
            gb += jnp.where(same, turned[0:b, at + TOP:at + TOP + 1], 0.0)
        hit[i * b:(i + 1) * b, :] = hb
        gsel_ref[i * b:(i + 1) * b, :] = gb
    r0 = lax.broadcasted_iota(jnp.int32, (GROUP, GROUP), 0)
    r1 = lax.broadcasted_iota(jnp.int32, (GROUP, GROUP), 1)
    before = jnp.where(r1 < r0, 1.0, 0.0)
    before_blk = jnp.where(r1 // b == r0 // b, before, 0.0).astype(BF16)
    before = before.astype(BF16)
    for g in range(nblk * b // GROUP):
        sl = slice(g * GROUP, (g + 1) * GROUP)
        rank = jnp.dot(before_blk, hit[sl, :].astype(BF16), preferred_element_type=F32)
        keep = jnp.where(rank < cap, hit[sl, :], 0.0)
        at = jnp.dot(before, keep.astype(BF16), preferred_element_type=F32)
        key = jnp.where(keep > 0.0, at, -1.0)
        key_ref[sl, :] = key
        krow_ref[:, sl] = key.T[0:8]
        cnt_ref[g:g + 1, :] = jnp.sum(keep, axis=0, keepdims=True).astype(jnp.int32)

    fwd = list(order[:-1])
    for i in range(n if n else 1, nw):
        shared(i)
        if i >= nw - 6:
            o = fwd.pop(0)
            send(o).wait_recv()
            forward(o).start()
            store(o, c).start()
    for o in fwd:
        send(o).wait_recv()
        forward(o).start()
        store(o, c).start()
    store(0, c).start()
    send(0).wait_recv()
    store(0, 1 - c).start()
    for o in order[:-1]:
        forward(o).wait_recv()
        store(o, 1 - c).start()
    for o in range(8):
        send(o).wait_send()
        store(o, c).wait()
        store(o, 1 - c).wait()
        if o:
            forward(o).wait_send()
    for o in range(1, 16):
        m_send(o).wait_send()


def _row(ref):
    return jnp.concatenate([ref[i:i + 1, :] for i in range(ref.shape[0])], axis=1)


def _front(x, k, v, lens, idx, gates, ln1, ln2, wq, wo, ws1, ws3):
    b, d = x.shape
    nqk, fs = wq.shape[1], ws1.shape[1]
    rows = k.shape[1] * k.shape[2]
    nk = 8
    ndev = 16
    k = k.reshape(nk, b // nk, rows, 128)
    v = v.reshape(nk, b // nk, rows, 128)
    nh = nqk // 128
    t = ndev * b
    return pl.pallas_call(
        functools.partial(_front_kernel, b - b // 8),
        out_shape=[jax.ShapeDtypeStruct((b, d), BF16), jax.ShapeDtypeStruct((ndev, b, d), BF16),
                   jax.ShapeDtypeStruct((b, fs), BF16), jax.ShapeDtypeStruct((t, 128), F32),
                   jax.ShapeDtypeStruct((t, 128), F32), jax.ShapeDtypeStruct((8, t), F32),
                   jax.ShapeDtypeStruct((t // GROUP, 128), jnp.int32)],
        in_specs=[VMEM] * 5 + [SMEM] + [HBM] * 6,
        out_specs=[VMEM, HBM] + [VMEM] * 5,
        scratch_shapes=[
            pltpu.VMEM((RING, d, CH), BF16),
            pltpu.VMEM((nk, b // nk, rows, 128), BF16),
            pltpu.VMEM((nk, b // nk, rows, 128), BF16),
            pltpu.VMEM((b * nh, 128), F32),
            pltpu.VMEM((b // 4, nh, rows), F32),
            pltpu.VMEM((b, nqk), BF16),
            pltpu.VMEM((b, d), BF16),
            pltpu.VMEM((ndev, b, d), BF16),
            pltpu.VMEM((2 * TOP, 128), F32),
            pltpu.VMEM((ndev, 2 * TOP, 128), F32),
            pltpu.VMEM((t, 128), F32),
            DMA((RING,)), DMA((nk,)), DMA((nk,)), DMA((16,)),
            DMA((8,)), DMA((8,)), DMA((8,)), DMA((8,)), DMA((16,)), DMA((16,)),
        ],
        compiler_params=pltpu.CompilerParams(vmem_limit_bytes=63 * 2 ** 20, collective_id=0, has_side_effects=True),
        name="front",
    )(x, ln1.reshape(d // 128, 128), ln2.reshape(d // 128, 128), idx.T, gates.T, lens, wq, k, v, wo, ws1, ws3)


SMALL = 32


def _expert_kernel(big, u_hbm, key_ref, gsel_ref, krow, cnt, w1_hbm, w3_hbm, w2_hbm, p_ref,
                   u_v, w1_v, w3_v, w2_v, kcol, gcol, mid, order, u_sem, w_sem):
    t, d = u_v.shape
    ng = t // GROUP
    u_copy = pltpu.make_async_copy(u_hbm, u_v, u_sem)
    u_copy.start()
    for e in range(EDEV):
        n = cnt[0, e] + cnt[1, e]
        rank = 0
        for f in range(EDEV):
            if f != e:
                m = cnt[0, f] + cnt[1, f]
                rank += ((m >= n) if f < e else (m > n)).astype(jnp.int32)
        order[rank] = e

    def copy(i, hbm, vm, k):
        s = lax.rem(i, 2)
        return pltpu.make_async_copy(hbm.at[order[i]], vm.at[s], w_sem.at[s, k])

    def w1_copy(i):
        return copy(i, w1_hbm, w1_v, 0)

    def w3_copy(i):
        return copy(i, w3_hbm, w3_v, 1)

    def w2_copy(i):
        return copy(i, w2_hbm, w2_v, 2)

    for i in range(2):
        w1_copy(i).start()
        w3_copy(i).start()
        w2_copy(i).start()
    p_ref[...] = jnp.zeros_like(p_ref)
    for e in range(EDEV):
        kcol[e] = jnp.broadcast_to(key_ref[:, e:e + 1], (t, 128))
        gcol[e] = jnp.broadcast_to(gsel_ref[:, e:e + 1], (t, 128))
    u_copy.wait()

    def tokens(g):
        return pl.ds(g * GROUP if isinstance(g, int) else pl.multiple_of(g * GROUP, GROUP), GROUP)

    def pick(e, g, n):
        r = lax.broadcasted_iota(jnp.int32, (n, GROUP), 0).astype(F32)
        sel = jnp.where(krow[pl.ds(e, 1), tokens(g)] == r, 1.0, 0.0).astype(BF16)
        return jnp.dot(sel, u_v[tokens(g), :], preferred_element_type=F32).astype(BF16)

    def put(e, g, n, out):
        tl = tokens(g)
        r = lax.broadcasted_iota(jnp.int32, (GROUP, 128), 1).astype(F32)
        key = kcol[e, tl]
        sel = jnp.concatenate([jnp.where(key == r + 128.0 * q, 1.0, 0.0) for q in range(-(-n // 128))], axis=1)
        sel = sel[:, :n].astype(BF16)
        gt = gcol[e, tl]
        for q in range(d // 256):
            cs = slice(q * 256, (q + 1) * 256)
            back = jnp.dot(sel, out[:, cs], preferred_element_type=F32)
            p_ref[tl, cs] += back * jnp.concatenate([gt, gt], axis=1)

    def up(rows, s):
        return _silu_mul(jnp.dot(rows, w1_v[s], preferred_element_type=F32),
                         jnp.dot(rows, w3_v[s], preferred_element_type=F32))

    def down(g, s):
        return jnp.dot(g, w2_v[s], preferred_element_type=F32).astype(BF16)

    @pl.loop(0, EDEV)
    def _(i):
        e, s = order[i], lax.rem(i, 2)
        most = jnp.maximum(cnt[0, e], cnt[1, e])
        few = jnp.logical_and(most > 0, most <= SMALL)
        w1_copy(i).wait()
        w3_copy(i).wait()

        @pl.when(few)
        def _():
            rows = jnp.concatenate([pick(e, g, SMALL) for g in range(ng)], axis=0)
            mid[0:ng * SMALL, :] = up(rows, s)

        @pl.when(most > SMALL)
        def _():
            @pl.loop(0, ng)
            def _(g):
                mid[pl.ds(pl.multiple_of(g * GROUP, GROUP), big), :] = up(pick(e, g, big), s)

        @pl.when(i + 2 < EDEV)
        def _():
            w1_copy(i + 2).start()
            w3_copy(i + 2).start()

        w2_copy(i).wait()

        @pl.when(few)
        def _():
            out = down(mid[0:ng * SMALL, :], s)
            for g in range(ng):
                put(e, g, SMALL, out[g * SMALL:(g + 1) * SMALL])

        @pl.when(most > SMALL)
        def _():
            @pl.loop(0, ng)
            def _(g):
                put(e, g, big, down(mid[pl.ds(pl.multiple_of(g * GROUP, GROUP), big), :], s))

        @pl.when(i + 2 < EDEV)
        def _():
            w2_copy(i + 2).start()


def _experts(u, key, gsel, krow, cnt, w1, w3, w2, blk):
    t, d = u.shape
    f = w1.shape[2]
    cap = blk - blk // 8
    return pl.pallas_call(
        functools.partial(_expert_kernel, cap * (GROUP // blk)),
        out_shape=jax.ShapeDtypeStruct((t, d), F32),
        in_specs=[HBM, VMEM, VMEM, VMEM, SMEM, HBM, HBM, HBM],
        out_specs=VMEM,
        scratch_shapes=[
            pltpu.VMEM((t, d), BF16),
            pltpu.VMEM((2, d, f), BF16),
            pltpu.VMEM((2, d, f), BF16),
            pltpu.VMEM((2, f, d), BF16),
            pltpu.VMEM((EDEV, t, 128), F32),
            pltpu.VMEM((EDEV, t, 128), F32),
            pltpu.VMEM((t, f), BF16),
            pltpu.SMEM((EDEV,), jnp.int32),
            DMA(()), DMA((2, 3)),
        ],
        compiler_params=pltpu.CompilerParams(vmem_limit_bytes=56 * 2 ** 20),
        name="experts",
    )(u, key, gsel, krow, cnt, w1, w3, w2)


COLS = ((0, 640), (640, 640), (1280, 768))


def _combine_kernel(p_hbm, g_ref, h_ref, w_hbm, y_ref,
                    acc, r0, r1, r2, r3, w_v, sh, w_sem, p_sem,
                    s0, q0, s1, q1, s2, q2, s3, q3):
    z, y, x, c = _place()
    nw, _, wn = w_v.shape

    def w_copy(i):
        return pltpu.make_async_copy(w_hbm.at[:, pl.ds(i * wn, wn)], w_v.at[i], w_sem.at[i])

    streams = [(p, half) for half in range(2) for p in range(3)]
    place = {0: x, 1: y, 2: z}

    def cols(p):
        return pl.ds(COLS[p][0], COLS[p][1])

    def rows(half):
        return pl.ds(half * 16, 16)

    def load(k):
        p, half = streams[k]
        return pltpu.make_async_copy(p_hbm.at[:, :, :, c, rows(half), cols(p)], acc.at[:, :, :, rows(half), cols(p)],
                                     p_sem.at[k])

    def swap(k):
        p, half = streams[k]
        return pltpu.make_async_remote_copy(
            p_hbm.at[:, :, :, 1 - c, rows(half), cols(p)], r0.at[:, :, :, rows(half), cols(p)], s0.at[k], q0.at[k],
            device_id=_dev(z, y, x, 1 - c), device_id_type=MESH)

    def region(ref, p, half, step, mine):
        ix = [pl.ds(0, 2)] * 3
        for s in range(step):
            dim = (p + s) % 3
            v = place[dim]
            ix[2 - dim] = v if (s < step - 1 or mine) else 1 - v
        return ref.at[ix[0], ix[1], ix[2], rows(half), cols(p)]

    def landing(p, half, step):
        ref = (r1, r2, r3)[step - 1]
        if step == 1:
            return ref.at[:, :, rows(half), cols(p)]
        if step == 2:
            return ref.at[:, rows(half), cols(p)]
        return ref.at[rows(half), cols(p)]

    def hop(k, step):
        p, half = streams[k]
        dim = (p + step - 1) % 3
        o = [z, y, x]
        o[2 - dim] = 1 - o[2 - dim]
        send, recv = ((s1, q1), (s2, q2), (s3, q3))[step - 1]
        return pltpu.make_async_remote_copy(
            region(acc, p, half, step, False), landing(p, half, step), send.at[k], recv.at[k],
            device_id=_dev(*o, c), device_id_type=MESH)

    for k in range(6):
        load(k).start()
    barrier = pltpu.get_barrier_semaphore()
    pl.semaphore_signal(barrier, inc=1, device_id=_dev(z, y, x, 1 - c), device_id_type=MESH)
    for d in (1, 2, 4):
        pl.semaphore_signal(barrier, inc=1, device_id=_dev(*_offset((z, y, x), d), c), device_id_type=MESH)
    pl.semaphore_wait(barrier, 4)
    for k in range(6):
        swap(k).start()
    for i in range(nw):
        w_copy(i).start()

    def shared(i):
        w_copy(i).wait()
        cs = slice(i * wn, (i + 1) * wn)
        sh[:, cs] = jnp.dot(g_ref[...], w_v[i], preferred_element_type=F32) + h_ref[:, cs].astype(F32)

    for k in range(6):
        p, half = streams[k]
        load(k).wait()
        swap(k).wait_recv()
        rs, cs = slice(half * 16, half * 16 + 16), slice(COLS[p][0], COLS[p][0] + COLS[p][1])
        acc[:, :, :, rs, cs] += r0[:, :, :, rs, cs]
        hop(k, 1).start()
    shared(0)
    for k in range(6):
        p, half = streams[k]
        hop(k, 1).wait_recv()
        v = region(acc, p, half, 1, True)
        v[...] += landing(p, half, 1)[...]
        hop(k, 2).start()
    shared(1)
    shared(2)
    for k in range(6):
        p, half = streams[k]
        hop(k, 2).wait_recv()
        v = region(acc, p, half, 2, True)
        v[...] += landing(p, half, 2)[...]
        hop(k, 3).start()
    for i in range(3, nw):
        shared(i)
    for k in range(6):
        p, half = streams[k]
        hop(k, 3).wait_recv()
        v = region(acc, p, half, 3, True)
        tot = v[...] + landing(p, half, 3)[...]
        rs, cs = slice(half * 16, half * 16 + 16), slice(COLS[p][0], COLS[p][0] + COLS[p][1])
        y_ref[rs, cs] = (sh[rs, cs] + tot).astype(BF16)
    for k in range(6):
        swap(k).wait_send()
        for step in (1, 2, 3):
            hop(k, step).wait_send()


def _combine(part, g, h, ws2):
    b, d = h.shape
    fs = ws2.shape[0]
    nw = 8
    part = part.reshape(2, 2, 2, 2, b, d)
    return pl.pallas_call(
        _combine_kernel,
        out_shape=jax.ShapeDtypeStruct((b, d), BF16),
        in_specs=[HBM, VMEM, VMEM, HBM],
        out_specs=VMEM,
        scratch_shapes=[
            pltpu.VMEM((2, 2, 2, b, d), F32),
            pltpu.VMEM((2, 2, 2, b, d), F32),
            pltpu.VMEM((2, 2, b, d), F32),
            pltpu.VMEM((2, b, d), F32),
            pltpu.VMEM((b, d), F32),
            pltpu.VMEM((nw, fs, d // nw), BF16),
            pltpu.VMEM((b, d), F32),
            DMA((nw,)), DMA((6,)),
            DMA((6,)), DMA((6,)), DMA((6,)), DMA((6,)), DMA((6,)), DMA((6,)), DMA((6,)), DMA((6,)),
        ],
        compiler_params=pltpu.CompilerParams(vmem_limit_bytes=62 * 2 ** 20, collective_id=1, has_side_effects=True),
        name="combine",
    )(part, g, h, ws2)


def solution(mesh):
    def body(x, kv_k, kv_v, lens, idx, gates, ln1, wq, wo, ln2, ws1, ws3, ws2, w1, w3, w2):
        b, d = x.shape
        h, uall, g, key, gsel, krow, cnt = _front(x, kv_k, kv_v, lens, idx, gates, ln1, ln2, wq, wo, ws1, ws3)
        part = _experts(uall.reshape(16 * b, d), key, gsel, krow, cnt, w1, w3, w2, b)
        return _combine(part, g, h, ws2)

    rows = P(GRP)
    rep = P()
    return jax.shard_map(
        body, mesh=mesh,
        in_specs=(rows, rows, rows, rows, rows, rows, rep, rep, rep, rep, rep, rep, rep, rows, rows, rows),
        out_specs=rows, check_vma=False)
```

time: 126 us -> 111 us (0.88)
  Pallas kernels: 120 us -> 110 us
  local copies, waits for them, and re-layouts: 5.06 us -> 1.57 us
  other arithmetic: 1.36 us -> 0 us
    pallas_call x3 -> x2, Pallas kernels: 86.1 us -> 72.9 us  [the longest x1 43.2 us: _front(): pl.pallas_call(functools.partial(_front_kernel, b - b // 8), out_shape=[j...]
    pallas_call x1, Pallas kernels: 33.6 us -> 36.7 us  [_combine(): pl.pallas_call(_combine_kernel, out_shape=jax.ShapeDtypeStruct((b, d), BF...]
    reshape x2 -> x0, local copies, waits for them, and re-layouts: 2.57 us -> none  [the longest x1 1.28 us: _attention(): ln1.reshape(1, d)]
where the time goes in v1:
time: 111 us
  Pallas kernels  110 us (99%)
  local copies, waits for them, and re-layouts  1.57 us (1%)
    pallas_call x1, Pallas kernels, _front(): pl.pallas_call(functools.partial(_front_kernel, b - b // 8), out_shape=[j...  43.2 us
    pallas_call x1, Pallas kernels, _combine(): pl.pallas_call(_combine_kernel, out_shape=jax.ShapeDtypeStruct((b, d), BF...  36.7 us
    pallas_call x1, Pallas kernels, _experts(): pl.pallas_call(functools.partial(_expert_kernel, cap * (GROUP // blk)), o...  29.6 us

profile of v1, /device:TPU:0, one launch (start us, length us, event | category | flops | bytes accessed | tf_op | source)
XLA Modules:
  0.0 111.2 jit_solution(9459137246422968823)
XLA Ops:
  0.0 43.2 %front.1 = (bf16[32,2048]{1,0:T(8,128)(2,1)}, bf16[16,32,2048]{2,1,0:T(8,128)(2,1)}, bf16[32,5632]{1,0:T(8,128)(2,1)}, f32[512,128]{1,0:T(8,128)}, f32[512,128]{...) custom-call(bf16[32,2048]{1,0:T(8,128)(2,1)} %x_ref.1, bf16[16,128]{1,0:T(8,128)(2,1)} %bitcast.12, ...), custom_call_target="tpu_custom_call" | custom-call | tf_op jit(solution)/shard_map/front/pallas_call | solution.py:290
  43.2 29.6 %experts.1 = f32[512,2048]{1,0:T(8,128)} custom-call(bf16[512,2048]{1,0:T(8,128)(2,1)} %bitcast.11, f32[512,128]{1,0:T(8,128)} %get-tuple-element.13.key_ref, f32[512,128]{1,0:T(8,128)} %get-tuple-element.14.gsel_ref, f32[8,512]{1,0:T(8,128)} %get-tuple-element.15.krow, s32[2,128]{1,0:T(2,128)} %get-tuple-element.16.cnt, bf16[4,2048,1408]{2,1,0:T(8,128)(2,1)} %w1_hbm.1, ...), custom_call_target="tpu_custom_call" | custom-call | tf_op jit(solution)/shard_map/experts/pallas_call | solution.py:433
  72.9 36.7 %combine.1 = bf16[32,2048]{1,0:T(8,128)(2,1)} custom-call(f32[2,2,2,2,32,2048]{5,4,3,2,1,0:T(8,128)} %bitcast.8, bf16[32,5632]{1,0:T(8,128)(2,1)} %get-tuple-element.17.g_ref, bf16[32,2048]{1,0:T(8,128)(2,1)} %get-tuple-element.18.h_ref, bf16[5632,2048]{1,0:T(8,128)(2,1)} %w_hbm.1), custom_call_target="tpu_custom_call" | custom-call | tf_op jit(solution)/shard_map/combine/pallas_call | solution.py:571
  109.6 1.6 %copy.18 = bf16[32,2048]{1,0:T(8,128)(2,1)} copy(bf16[32,2048]{1,0:T(8,128)(2,1)} %combine.1) | data formatting | bytes 262144

commit v2 on v1

--- a/solution.py
+++ b/solution.py
@@ -54,8 +54,8 @@
 
 
 def _front_kernel(cap, x_ref, ln1_ref, ln2_ref, idx_ref, gate_ref, lens_ref, wq_hbm, k_hbm, v_hbm, wo_hbm, ws1_hbm,
-                  ws3_hbm, h_ref, uall_hbm, g_ref, key_ref, gsel_ref, krow_ref, cnt_ref,
-                  ring, k_v, v_v, qs, sc, ob, us, ua, ms, ma, hit,
+                  ws3_hbm, h_ref, hall_hbm, g_ref, key_ref, gsel_ref, krow_ref, cnt_ref,
+                  ring, k_v, v_v, qs, sc, ob, us, ha, ms, ma, hit,
                   r_sem, k_sem, v_sem, out_sem, us_send, us_recv, uf_send, uf_recv, ms_send, ms_recv):
     b, d = x_ref.shape
     nqk = wq_hbm.shape[1]
@@ -103,12 +103,13 @@
     def _(i):
         k_copy(i).start()
         v_copy(i).start()
-        o_copy(i).start()
         q_copy(i).wait()
         q = jnp.dot(a, ring[i], preferred_element_type=F32).astype(BF16).astype(F32)
         for j in range(CH // 128):
             qs[pl.ds(i * (CH // 128) + j, b, stride=nh), :] = q[:, j * 128:(j + 1) * 128]
 
+    for i in range(2 * d // CH):
+        o_copy(i).start()
     pl.semaphore_wait(barrier, 15)
 
     def m_send(o):
@@ -158,8 +159,26 @@
 
     no = d // CH
 
-    @pl.loop(0, no)
-    def _(i):
+    def send(o, i):
+        dev = _dev(*_offset((z, y, x), o), c) if o else _dev(z, y, x, 1 - c)
+        return pltpu.make_async_remote_copy(h_ref.at[:, cols(i)], ha.at[me, :, cols(i)], us_send.at[o, i],
+                                            us_recv.at[o, i], device_id=dev, device_id_type=MESH)
+
+    def source(o, core):
+        oz, oy, ox = _offset((z, y, x), o)
+        return ((oz * 2 + oy) * 2 + ox) * 2 + core
+
+    def forward(o, i):
+        at = ha.at[source(o, c), :, cols(i)]
+        return pltpu.make_async_remote_copy(at, at, uf_send.at[o, i], uf_recv.at[o, i],
+                                            device_id=_dev(z, y, x, 1 - c), device_id_type=MESH)
+
+    def store(o, core):
+        src = source(o, core)
+        return pltpu.make_async_copy(ha.at[src], hall_hbm.at[src], out_sem.at[2 * o + (0 if core is c else 1)])
+
+    order = (7, 6, 5, 3, 4, 2, 1, 0)
+    for i in range(no):
         acc = x_ref[:, cols(i)].astype(F32)
         attn = jnp.zeros((b, CH), F32)
         for t in range(2):
@@ -168,8 +187,11 @@
         h_ref[:, cols(i)] = (acc + attn).astype(BF16)
         for cp in w_copies(ahead + i):
             cp.start()
+        for o in order:
+            send(o, i).start()
 
     ahead += no
+    ha[me] = h_ref[...]
     us[...] = _rms(h_ref[...].astype(F32), _row(ln2_ref))
 
     def shared(i):
@@ -183,28 +205,6 @@
 
     shared(0)
 
-    def send(o):
-        dev = _dev(*_offset((z, y, x), o), c) if o else _dev(z, y, x, 1 - c)
-        return pltpu.make_async_remote_copy(us, ua.at[me], us_send.at[o], us_recv.at[o], device_id=dev,
-                                            device_id_type=MESH)
-
-    def source(o, core):
-        oz, oy, ox = _offset((z, y, x), o)
-        return ((oz * 2 + oy) * 2 + ox) * 2 + core
-
-    def forward(o):
-        src = source(o, c)
-        return pltpu.make_async_remote_copy(ua.at[src], ua.at[src], uf_send.at[o], uf_recv.at[o],
-                                            device_id=_dev(z, y, x, 1 - c), device_id_type=MESH)
-
-    def store(o, core):
-        src = source(o, core)
-        return pltpu.make_async_copy(ua.at[src], uall_hbm.at[src], out_sem.at[2 * o + (0 if core is c else 1)])
-
-    order = (7, 6, 5, 3, 4, 2, 1, 0)
-    for o in order:
-        send(o).start()
-    ua[me] = us[...]
     n = 0
     while ahead < nw:
         for cp in w_copies(ahead):
@@ -245,30 +245,31 @@
         krow_ref[:, sl] = key.T[0:8]
         cnt_ref[g:g + 1, :] = jnp.sum(keep, axis=0, keepdims=True).astype(jnp.int32)
 
-    fwd = list(order[:-1])
     for i in range(n if n else 1, nw):
         shared(i)
-        if i >= nw - 6:
-            o = fwd.pop(0)
-            send(o).wait_recv()
-            forward(o).start()
-            store(o, c).start()
-    for o in fwd:
-        send(o).wait_recv()
-        forward(o).start()
-        store(o, c).start()
-    store(0, c).start()
-    send(0).wait_recv()
-    store(0, 1 - c).start()
+        at = {2: 0, 4: 1, 6: 2, 8: 3}.get(i)
+        if at is not None:
+            for o in order[:-1]:
+                send(o, at).wait_recv()
+                forward(o, at).start()
+                if at == no - 1:
+                    store(o, c).start()
+            if at == no - 1:
+                store(0, c).start()
+                for t in range(no):
+                    send(0, t).wait_recv()
+                store(0, 1 - c).start()
     for o in order[:-1]:
-        forward(o).wait_recv()
+        for t in range(no):
+            forward(o, t).wait_recv()
         store(o, 1 - c).start()
     for o in range(8):
-        send(o).wait_send()
+        for t in range(no):
+            send(o, t).wait_send()
+            if o:
+                forward(o, t).wait_send()
         store(o, c).wait()
         store(o, 1 - c).wait()
-        if o:
-            forward(o).wait_send()
     for o in range(1, 16):
         m_send(o).wait_send()
 
@@ -308,7 +309,7 @@
             pltpu.VMEM((ndev, 2 * TOP, 128), F32),
             pltpu.VMEM((t, 128), F32),
             DMA((RING,)), DMA((nk,)), DMA((nk,)), DMA((16,)),
-            DMA((8,)), DMA((8,)), DMA((8,)), DMA((8,)), DMA((16,)), DMA((16,)),
+            DMA((8, d // CH)), DMA((8, d // CH)), DMA((8, d // CH)), DMA((8, d // CH)), DMA((16,)), DMA((16,)),
         ],
         compiler_params=pltpu.CompilerParams(vmem_limit_bytes=63 * 2 ** 20, collective_id=0, has_side_effects=True),
         name="front",
@@ -318,11 +319,11 @@
 SMALL = 32
 
 
-def _expert_kernel(big, u_hbm, key_ref, gsel_ref, krow, cnt, w1_hbm, w3_hbm, w2_hbm, p_ref,
-                   u_v, w1_v, w3_v, w2_v, kcol, gcol, mid, order, u_sem, w_sem):
+def _expert_kernel(big, blk, h_hbm, ln2_ref, key_ref, gsel_ref, krow, cnt, w1_hbm, w3_hbm, w2_hbm, p_ref,
+                   u_v, xs, zs, w1_v, w3_v, w2_v, kcol, gcol, mid, order, u_sem, w_sem):
     t, d = u_v.shape
     ng = t // GROUP
-    u_copy = pltpu.make_async_copy(u_hbm, u_v, u_sem)
+    u_copy = pltpu.make_async_copy(h_hbm, u_v, u_sem)
     u_copy.start()
     for e in range(EDEV):
         n = cnt[0, e] + cnt[1, e]
@@ -355,6 +356,12 @@
         kcol[e] = jnp.broadcast_to(key_ref[:, e:e + 1], (t, 128))
         gcol[e] = jnp.broadcast_to(gsel_ref[:, e:e + 1], (t, 128))
     u_copy.wait()
+    ln2 = _row(ln2_ref)
+
+    @pl.loop(0, t // blk)
+    def _(i):
+        at = pl.ds(pl.multiple_of(i * blk, blk), blk)
+        u_v[at, :] = _rms(u_v[at, :].astype(F32), ln2)
 
     def tokens(g):
         return pl.ds(g * GROUP if isinstance(g, int) else pl.multiple_of(g * GROUP, GROUP), GROUP)
@@ -376,9 +383,8 @@
             back = jnp.dot(sel, out[:, cs], preferred_element_type=F32)
             p_ref[tl, cs] += back * jnp.concatenate([gt, gt], axis=1)
 
-    def up(rows, s):
-        return _silu_mul(jnp.dot(rows, w1_v[s], preferred_element_type=F32),
-                         jnp.dot(rows, w3_v[s], preferred_element_type=F32))
+    def slots(g):
+        return pl.ds(pl.multiple_of(g * big, 16), big)
 
     def down(g, s):
         return jnp.dot(g, w2_v[s], preferred_element_type=F32).astype(BF16)
@@ -388,70 +394,103 @@
         e, s = order[i], lax.rem(i, 2)
         most = jnp.maximum(cnt[0, e], cnt[1, e])
         few = jnp.logical_and(most > 0, most <= SMALL)
-        w1_copy(i).wait()
-        w3_copy(i).wait()
+        many = most > SMALL
+        both = slice(0, ng * SMALL)
 
         @pl.when(few)
         def _():
-            rows = jnp.concatenate([pick(e, g, SMALL) for g in range(ng)], axis=0)
-            mid[0:ng * SMALL, :] = up(rows, s)
-
-        @pl.when(most > SMALL)
+            for g in range(ng):
+                xs[g * SMALL:(g + 1) * SMALL, :] = pick(e, g, SMALL)
+
+        @pl.when(many)
         def _():
             @pl.loop(0, ng)
             def _(g):
-                mid[pl.ds(pl.multiple_of(g * GROUP, GROUP), big), :] = up(pick(e, g, big), s)
+                xs[slots(g), :] = pick(e, g, big)
+
+        w1_copy(i).wait()
+
+        @pl.when(few)
+        def _():
+            zs[both, :] = jnp.dot(xs[both, :], w1_v[s], preferred_element_type=F32)
+
+        @pl.when(many)
+        def _():
+            @pl.loop(0, ng)
+            def _(g):
+                zs[slots(g), :] = jnp.dot(xs[slots(g), :], w1_v[s], preferred_element_type=F32)
 
         @pl.when(i + 2 < EDEV)
         def _():
             w1_copy(i + 2).start()
+
+        w3_copy(i).wait()
+
+        @pl.when(few)
+        def _():
+            mid[both, :] = _silu_mul(zs[both, :], jnp.dot(xs[both, :], w3_v[s], preferred_element_type=F32))
+
+        @pl.when(many)
+        def _():
+            @pl.loop(0, ng)
+            def _(g):
+                mid[slots(g), :] = _silu_mul(
+                    zs[slots(g), :], jnp.dot(xs[slots(g), :], w3_v[s], preferred_element_type=F32))
+
+        @pl.when(i + 2 < EDEV)
+        def _():
             w3_copy(i + 2).start()
 
         w2_copy(i).wait()
 
         @pl.when(few)
         def _():
-            out = down(mid[0:ng * SMALL, :], s)
+            out = down(mid[both, :], s)
             for g in range(ng):
                 put(e, g, SMALL, out[g * SMALL:(g + 1) * SMALL])
 
-        @pl.when(most > SMALL)
+        @pl.when(many)
         def _():
             @pl.loop(0, ng)
             def _(g):
-                put(e, g, big, down(mid[pl.ds(pl.multiple_of(g * GROUP, GROUP), big), :], s))
+                put(e, g, big, down(mid[slots(g), :], s))
 
         @pl.when(i + 2 < EDEV)
         def _():
             w2_copy(i + 2).start()
 
 
-def _experts(u, key, gsel, krow, cnt, w1, w3, w2, blk):
-    t, d = u.shape
+def _experts(h, ln2, key, gsel, krow, cnt, w1, w3, w2, blk):
+    t, d = h.shape
     f = w1.shape[2]
-    cap = blk - blk // 8
+    big = (blk - blk // 8) * (GROUP // blk)
+    slots = big * (t // GROUP)
     return pl.pallas_call(
-        functools.partial(_expert_kernel, cap * (GROUP // blk)),
+        functools.partial(_expert_kernel, big, blk),
         out_shape=jax.ShapeDtypeStruct((t, d), F32),
-        in_specs=[HBM, VMEM, VMEM, VMEM, SMEM, HBM, HBM, HBM],
+        in_specs=[HBM, VMEM, VMEM, VMEM, VMEM, SMEM, HBM, HBM, HBM],
         out_specs=VMEM,
         scratch_shapes=[
             pltpu.VMEM((t, d), BF16),
+            pltpu.VMEM((slots, d), BF16),
+            pltpu.VMEM((slots, f), F32),
             pltpu.VMEM((2, d, f), BF16),
             pltpu.VMEM((2, d, f), BF16),
             pltpu.VMEM((2, f, d), BF16),
             pltpu.VMEM((EDEV, t, 128), F32),
             pltpu.VMEM((EDEV, t, 128), F32),
-            pltpu.VMEM((t, f), BF16),
+            pltpu.VMEM((slots, f), BF16),
             pltpu.SMEM((EDEV,), jnp.int32),
             DMA(()), DMA((2, 3)),
         ],
-        compiler_params=pltpu.CompilerParams(vmem_limit_bytes=56 * 2 ** 20),
+        compiler_params=pltpu.CompilerParams(vmem_limit_bytes=58 * 2 ** 20),
         name="experts",
-    )(u, key, gsel, krow, cnt, w1, w3, w2)
+    )(h, ln2.reshape(d // 128, 128), key, gsel, krow, cnt, w1, w3, w2)
 
 
 COLS = ((0, 640), (640, 640), (1280, 768))
+PARTS, ROWS = 4, 8
+NS = 3 * PARTS
 
 
 def _combine_kernel(p_hbm, g_ref, h_ref, w_hbm, y_ref,
@@ -463,14 +502,14 @@
     def w_copy(i):
         return pltpu.make_async_copy(w_hbm.at[:, pl.ds(i * wn, wn)], w_v.at[i], w_sem.at[i])
 
-    streams = [(p, half) for half in range(2) for p in range(3)]
+    streams = [(p, half) for half in range(PARTS) for p in range(3)]
     place = {0: x, 1: y, 2: z}
 
     def cols(p):
         return pl.ds(COLS[p][0], COLS[p][1])
 
     def rows(half):
-        return pl.ds(half * 16, 16)
+        return pl.ds(half * ROWS, ROWS)
 
     def load(k):
         p, half = streams[k]
@@ -509,14 +548,14 @@
             region(acc, p, half, step, False), landing(p, half, step), send.at[k], recv.at[k],
             device_id=_dev(*o, c), device_id_type=MESH)
 
-    for k in range(6):
+    for k in range(NS):
         load(k).start()
     barrier = pltpu.get_barrier_semaphore()
     pl.semaphore_signal(barrier, inc=1, device_id=_dev(z, y, x, 1 - c), device_id_type=MESH)
     for d in (1, 2, 4):
         pl.semaphore_signal(barrier, inc=1, device_id=_dev(*_offset((z, y, x), d), c), device_id_type=MESH)
     pl.semaphore_wait(barrier, 4)
-    for k in range(6):
+    for k in range(NS):
         swap(k).start()
     for i in range(nw):
         w_copy(i).start()
@@ -526,15 +565,15 @@
         cs = slice(i * wn, (i + 1) * wn)
         sh[:, cs] = jnp.dot(g_ref[...], w_v[i], preferred_element_type=F32) + h_ref[:, cs].astype(F32)
 
-    for k in range(6):
+    for k in range(NS):
         p, half = streams[k]
         load(k).wait()
         swap(k).wait_recv()
-        rs, cs = slice(half * 16, half * 16 + 16), slice(COLS[p][0], COLS[p][0] + COLS[p][1])
+        rs, cs = slice(half * ROWS, half * ROWS + ROWS), slice(COLS[p][0], COLS[p][0] + COLS[p][1])
         acc[:, :, :, rs, cs] += r0[:, :, :, rs, cs]
         hop(k, 1).start()
     shared(0)
-    for k in range(6):
+    for k in range(NS):
         p, half = streams[k]
         hop(k, 1).wait_recv()
         v = region(acc, p, half, 1, True)
@@ -542,7 +581,7 @@
         hop(k, 2).start()
     shared(1)
     shared(2)
-    for k in range(6):
+    for k in range(NS):
         p, half = streams[k]
         hop(k, 2).wait_recv()
         v = region(acc, p, half, 2, True)
@@ -550,14 +589,14 @@
         hop(k, 3).start()
     for i in range(3, nw):
         shared(i)
-    for k in range(6):
+    for k in range(NS):
         p, half = streams[k]
         hop(k, 3).wait_recv()
         v = region(acc, p, half, 3, True)
         tot = v[...] + landing(p, half, 3)[...]
-        rs, cs = slice(half * 16, half * 16 + 16), slice(COLS[p][0], COLS[p][0] + COLS[p][1])
+        rs, cs = slice(half * ROWS, half * ROWS + ROWS), slice(COLS[p][0], COLS[p][0] + COLS[p][1])
         y_ref[rs, cs] = (sh[rs, cs] + tot).astype(BF16)
-    for k in range(6):
+    for k in range(NS):
         swap(k).wait_send()
         for step in (1, 2, 3):
             hop(k, step).wait_send()
@@ -581,8 +620,8 @@
             pltpu.VMEM((b, d), F32),
             pltpu.VMEM((nw, fs, d // nw), BF16),
             pltpu.VMEM((b, d), F32),
-            DMA((nw,)), DMA((6,)),
-            DMA((6,)), DMA((6,)), DMA((6,)), DMA((6,)), DMA((6,)), DMA((6,)), DMA((6,)), DMA((6,)),
+            DMA((nw,)), DMA((NS,)),
+            DMA((NS,)), DMA((NS,)), DMA((NS,)), DMA((NS,)), DMA((NS,)), DMA((NS,)), DMA((NS,)), DMA((NS,)),
         ],
         compiler_params=pltpu.CompilerParams(vmem_limit_bytes=62 * 2 ** 20, collective_id=1, has_side_effects=True),
         name="combine",
@@ -592,8 +631,8 @@
 def solution(mesh):
     def body(x, kv_k, kv_v, lens, idx, gates, ln1, wq, wo, ln2, ws1, ws3, ws2, w1, w3, w2):
         b, d = x.shape
-        h, uall, g, key, gsel, krow, cnt = _front(x, kv_k, kv_v, lens, idx, gates, ln1, ln2, wq, wo, ws1, ws3)
-        part = _experts(uall.reshape(16 * b, d), key, gsel, krow, cnt, w1, w3, w2, b)
+        h, hall, g, key, gsel, krow, cnt = _front(x, kv_k, kv_v, lens, idx, gates, ln1, ln2, wq, wo, ws1, ws3)
+        part = _experts(hall.reshape(16 * b, d), ln2, key, gsel, krow, cnt, w1, w3, w2, b)
         return _combine(part, g, h, ws2)
 
     rows = P(GRP)

time: 111 us -> 110 us (level)
  Pallas kernels: 110 us -> 108 us
    pallas_call x1, Pallas kernels: 43.2 us -> 37 us  [_front(): pl.pallas_call(functools.partial(_front_kernel, b - b // 8), out_shape=[j...]
    pallas_call x1, Pallas kernels: 29.6 us -> 32.8 us  [_experts(): pl.pallas_call(functools.partial(_expert_kernel, big, blk), out_shape=jax...]
    pallas_call x1, Pallas kernels: 36.7 us -> 38.1 us  [_combine(): pl.pallas_call(_combine_kernel, out_shape=jax.ShapeDtypeStruct((b, d), BF...]
where the time goes in v2:
time: 110 us; the launch traced here: 109 us
  Pallas kernels  108 us (98%)
  local copies, waits for them, and re-layouts  1.57 us (1%)
    pallas_call x1, Pallas kernels, _combine(): pl.pallas_call(_combine_kernel, out_shape=jax.ShapeDtypeStruct((b, d), BF...  38.1 us
    pallas_call x1, Pallas kernels, _front(): pl.pallas_call(functools.partial(_front_kernel, b - b // 8), out_shape=[j...  37 us
    pallas_call x1, Pallas kernels, _experts(): pl.pallas_call(functools.partial(_expert_kernel, big, blk), out_shape=jax...  32.8 us

profile of v2, /device:TPU:0, one launch (start us, length us, event | category | flops | bytes accessed | tf_op | source)
XLA Modules:
  0.0 109.5 jit_solution(14241781155920840505)
XLA Ops:
  0.0 37.0 %front.1 = (bf16[32,2048]{1,0:T(8,128)(2,1)}, bf16[16,32,2048]{2,1,0:T(8,128)(2,1)}, bf16[32,5632]{1,0:T(8,128)(2,1)}, f32[512,128]{1,0:T(8,128)}, f32[512,128]{...) custom-call(bf16[32,2048]{1,0:T(8,128)(2,1)} %x_ref.1, bf16[16,128]{1,0:T(8,128)(2,1)} %bitcast.14, ...), custom_call_target="tpu_custom_call" | custom-call | tf_op jit(solution)/shard_map/front/pallas_call | solution.py:291
  37.0 32.8 %experts.1 = f32[512,2048]{1,0:T(8,128)} custom-call(bf16[512,2048]{1,0:T(8,128)(2,1)} %bitcast.11, bf16[16,128]{1,0:T(8,128)(2,1)} %bitcast.13, f32[512,128]{1,0:T(8,128)} %get-tuple-element.13.key_ref, f32[512,128]{1,0:T(8,128)} %get-tuple-element.14.gsel_ref, f32[8,512]{1,0:T(8,128)} %get-tuple-element.15.krow, s32[2,128]{1,0:T(2,128)} %get-tuple-element.16.cnt, ...), custom_call_target="tpu_custom_call" | custom-call | tf_op jit(solution)/shard_map/experts/pallas_call | solution.py:468
  69.8 38.1 %combine.1 = bf16[32,2048]{1,0:T(8,128)(2,1)} custom-call(f32[2,2,2,2,32,2048]{5,4,3,2,1,0:T(8,128)} %bitcast.8, bf16[32,5632]{1,0:T(8,128)(2,1)} %get-tuple-element.17.g_ref, bf16[32,2048]{1,0:T(8,128)(2,1)} %get-tuple-element.18.h_ref, bf16[5632,2048]{1,0:T(8,128)(2,1)} %w_hbm.1), custom_call_target="tpu_custom_call" | custom-call | tf_op jit(solution)/shard_map/combine/pallas_call | solution.py:610
  107.9 1.6 %copy.18 = bf16[32,2048]{1,0:T(8,128)(2,1)} copy(bf16[32,2048]{1,0:T(8,128)(2,1)} %combine.1) | data formatting | bytes 262144

commit v3 on v2

--- a/solution.py
+++ b/solution.py
@@ -49,20 +49,21 @@
 
 
 CH = 512
-RING = 18
+RING = 16
+LATE = 3
 GROUP = 256
 
 
 def _front_kernel(cap, x_ref, ln1_ref, ln2_ref, idx_ref, gate_ref, lens_ref, wq_hbm, k_hbm, v_hbm, wo_hbm, ws1_hbm,
-                  ws3_hbm, h_ref, hall_hbm, g_ref, key_ref, gsel_ref, krow_ref, cnt_ref,
-                  ring, k_v, v_v, qs, sc, ob, us, ha, ms, ma, hit,
+                  ws3_hbm, h_ref, us, uall_hbm, g_ref, key_ref, gsel_ref, krow_ref, cnt_ref,
+                  ring, k_v, v_v, qs, sc, ob, ha, ua, ms, ma, hit,
                   r_sem, k_sem, v_sem, out_sem, us_send, us_recv, uf_send, uf_recv, ms_send, ms_recv):
     b, d = x_ref.shape
     nqk = wq_hbm.shape[1]
     nh = nqk // 128
     nq = nqk // CH
     nk, kb, rows = k_v.shape[:3]
-    nw = ws1_hbm.shape[1] // CH
+    nw = ws1_hbm.shape[1] // CH - LATE
     z, y, x, c = _place()
     me = ((z * 2 + y) * 2 + x) * 2 + c
 
@@ -175,7 +176,7 @@
 
     def store(o, core):
         src = source(o, core)
-        return pltpu.make_async_copy(ha.at[src], hall_hbm.at[src], out_sem.at[2 * o + (0 if core is c else 1)])
+        return pltpu.make_async_copy(ua.at[src], uall_hbm.at[src], out_sem.at[2 * o + (0 if core is c else 1)])
 
     order = (7, 6, 5, 3, 4, 2, 1, 0)
     for i in range(no):
@@ -191,8 +192,8 @@
             send(o, i).start()
 
     ahead += no
-    ha[me] = h_ref[...]
-    us[...] = _rms(h_ref[...].astype(F32), _row(ln2_ref))
+    ln2 = _row(ln2_ref)
+    us[...] = _rms(h_ref[...].astype(F32), ln2)
 
     def shared(i):
         c1, c3 = w_copies(i)
@@ -203,6 +204,7 @@
         z3 = jnp.dot(us[...], ring[s + 1], preferred_element_type=F32)
         g_ref[:, cols(i)] = _silu_mul(z1, z3)
 
+    ua[me] = us[...]
     shared(0)
 
     n = 0
@@ -247,21 +249,28 @@
 
     for i in range(n if n else 1, nw):
         shared(i)
-        at = {2: 0, 4: 1, 6: 2, 8: 3}.get(i)
+        at = {1: 0, 3: 1, 5: 2, 7: 3}.get(i)
         if at is not None:
             for o in order[:-1]:
                 send(o, at).wait_recv()
                 forward(o, at).start()
-                if at == no - 1:
-                    store(o, c).start()
-            if at == no - 1:
-                store(0, c).start()
-                for t in range(no):
-                    send(0, t).wait_recv()
-                store(0, 1 - c).start()
+
+    def normalise(o, core):
+        src = source(o, core)
+        ua[src] = _rms(ha[src].astype(F32), ln2)
+
+    for o in order[:-1]:
+        normalise(o, c)
+    for o in range(8):
+        store(o, c).start()
+    for t in range(no):
+        send(0, t).wait_recv()
     for o in order[:-1]:
         for t in range(no):
             forward(o, t).wait_recv()
+    for o in range(8):
+        normalise(o, 1 - c)
+    for o in range(8):
         store(o, 1 - c).start()
     for o in range(8):
         for t in range(no):
@@ -280,7 +289,7 @@
 
 def _front(x, k, v, lens, idx, gates, ln1, ln2, wq, wo, ws1, ws3):
     b, d = x.shape
-    nqk, fs = wq.shape[1], ws1.shape[1]
+    nqk, fs = wq.shape[1], ws1.shape[1] - LATE * CH
     rows = k.shape[1] * k.shape[2]
     nk = 8
     ndev = 16
@@ -290,12 +299,12 @@
     t = ndev * b
     return pl.pallas_call(
         functools.partial(_front_kernel, b - b // 8),
-        out_shape=[jax.ShapeDtypeStruct((b, d), BF16), jax.ShapeDtypeStruct((ndev, b, d), BF16),
+        out_shape=[jax.ShapeDtypeStruct((b, d), BF16)] * 2 + [jax.ShapeDtypeStruct((ndev, b, d), BF16),
                    jax.ShapeDtypeStruct((b, fs), BF16), jax.ShapeDtypeStruct((t, 128), F32),
                    jax.ShapeDtypeStruct((t, 128), F32), jax.ShapeDtypeStruct((8, t), F32),
                    jax.ShapeDtypeStruct((t // GROUP, 128), jnp.int32)],
         in_specs=[VMEM] * 5 + [SMEM] + [HBM] * 6,
-        out_specs=[VMEM, HBM] + [VMEM] * 5,
+        out_specs=[VMEM, VMEM, HBM] + [VMEM] * 5,
         scratch_shapes=[
             pltpu.VMEM((RING, d, CH), BF16),
             pltpu.VMEM((nk, b // nk, rows, 128), BF16),
@@ -303,7 +312,7 @@
             pltpu.VMEM((b * nh, 128), F32),
             pltpu.VMEM((b // 4, nh, rows), F32),
             pltpu.VMEM((b, nqk), BF16),
-            pltpu.VMEM((b, d), BF16),
+            pltpu.VMEM((ndev, b, d), BF16),
             pltpu.VMEM((ndev, b, d), BF16),
             pltpu.VMEM((2 * TOP, 128), F32),
             pltpu.VMEM((ndev, 2 * TOP, 128), F32),
@@ -319,11 +328,11 @@
 SMALL = 32
 
 
-def _expert_kernel(big, blk, h_hbm, ln2_ref, key_ref, gsel_ref, krow, cnt, w1_hbm, w3_hbm, w2_hbm, p_ref,
-                   u_v, xs, zs, w1_v, w3_v, w2_v, kcol, gcol, mid, order, u_sem, w_sem):
+def _expert_kernel(big, u_hbm, key_ref, gsel_ref, krow, cnt, w1_hbm, w3_hbm, w2_hbm, p_ref,
+                   u_v, xs, zs, w1_v, w3_v, w2_v, mid, order, u_sem, w_sem):
     t, d = u_v.shape
     ng = t // GROUP
-    u_copy = pltpu.make_async_copy(h_hbm, u_v, u_sem)
+    u_copy = pltpu.make_async_copy(u_hbm, u_v, u_sem)
     u_copy.start()
     for e in range(EDEV):
         n = cnt[0, e] + cnt[1, e]
@@ -352,16 +361,8 @@
         w3_copy(i).start()
         w2_copy(i).start()
     p_ref[...] = jnp.zeros_like(p_ref)
-    for e in range(EDEV):
-        kcol[e] = jnp.broadcast_to(key_ref[:, e:e + 1], (t, 128))
-        gcol[e] = jnp.broadcast_to(gsel_ref[:, e:e + 1], (t, 128))
     u_copy.wait()
-    ln2 = _row(ln2_ref)
-
-    @pl.loop(0, t // blk)
-    def _(i):
-        at = pl.ds(pl.multiple_of(i * blk, blk), blk)
-        u_v[at, :] = _rms(u_v[at, :].astype(F32), ln2)
+    lane = lax.broadcasted_iota(jnp.int32, (GROUP, 128), 1)
 
     def tokens(g):
         return pl.ds(g * GROUP if isinstance(g, int) else pl.multiple_of(g * GROUP, GROUP), GROUP)
@@ -374,14 +375,14 @@
     def put(e, g, n, out):
         tl = tokens(g)
         r = lax.broadcasted_iota(jnp.int32, (GROUP, 128), 1).astype(F32)
-        key = kcol[e, tl]
+        key = jnp.sum(jnp.where(lane == e, key_ref[tl, :], 0.0), axis=1, keepdims=True)
         sel = jnp.concatenate([jnp.where(key == r + 128.0 * q, 1.0, 0.0) for q in range(-(-n // 128))], axis=1)
         sel = sel[:, :n].astype(BF16)
-        gt = gcol[e, tl]
+        gt = jnp.sum(jnp.where(lane == e, gsel_ref[tl, :], 0.0), axis=1, keepdims=True)
         for q in range(d // 256):
             cs = slice(q * 256, (q + 1) * 256)
             back = jnp.dot(sel, out[:, cs], preferred_element_type=F32)
-            p_ref[tl, cs] += back * jnp.concatenate([gt, gt], axis=1)
+            p_ref[tl, cs] += back * gt
 
     def slots(g):
         return pl.ds(pl.multiple_of(g * big, 16), big)
@@ -460,15 +461,15 @@
             w2_copy(i + 2).start()
 
 
-def _experts(h, ln2, key, gsel, krow, cnt, w1, w3, w2, blk):
-    t, d = h.shape
+def _experts(u, key, gsel, krow, cnt, w1, w3, w2, blk):
+    t, d = u.shape
     f = w1.shape[2]
     big = (blk - blk // 8) * (GROUP // blk)
     slots = big * (t // GROUP)
     return pl.pallas_call(
-        functools.partial(_expert_kernel, big, blk),
+        functools.partial(_expert_kernel, big),
         out_shape=jax.ShapeDtypeStruct((t, d), F32),
-        in_specs=[HBM, VMEM, VMEM, VMEM, VMEM, SMEM, HBM, HBM, HBM],
+        in_specs=[HBM, VMEM, VMEM, VMEM, SMEM, HBM, HBM, HBM],
         out_specs=VMEM,
         scratch_shapes=[
             pltpu.VMEM((t, d), BF16),
@@ -477,15 +478,13 @@
             pltpu.VMEM((2, d, f), BF16),
             pltpu.VMEM((2, d, f), BF16),
             pltpu.VMEM((2, f, d), BF16),
-            pltpu.VMEM((EDEV, t, 128), F32),
-            pltpu.VMEM((EDEV, t, 128), F32),
             pltpu.VMEM((slots, f), BF16),
             pltpu.SMEM((EDEV,), jnp.int32),
             DMA(()), DMA((2, 3)),
         ],
-        compiler_params=pltpu.CompilerParams(vmem_limit_bytes=58 * 2 ** 20),
+        compiler_params=pltpu.CompilerParams(vmem_limit_bytes=55 * 2 ** 20),
         name="experts",
-    )(h, ln2.reshape(d // 128, 128), key, gsel, krow, cnt, w1, w3, w2)
+    )(u, key, gsel, krow, cnt, w1, w3, w2)
 
 
 COLS = ((0, 640), (640, 640), (1280, 768))
@@ -493,8 +492,8 @@
 NS = 3 * PARTS
 
 
-def _combine_kernel(p_hbm, g_ref, h_ref, w_hbm, y_ref,
-                    acc, r0, r1, r2, r3, w_v, sh, w_sem, p_sem,
+def _combine_kernel(p_ref, g_ref, h_ref, u_ref, ws1_hbm, ws3_hbm, w_hbm, y_ref,
+                    acc, r0, r1, r2, r3, w_v, a_v, b_v, late, sh, w_sem, a_sem, b_sem,
                     s0, q0, s1, q1, s2, q2, s3, q3):
     z, y, x, c = _place()
     nw, _, wn = w_v.shape
@@ -511,15 +510,18 @@
     def rows(half):
         return pl.ds(half * ROWS, ROWS)
 
-    def load(k):
-        p, half = streams[k]
-        return pltpu.make_async_copy(p_hbm.at[:, :, :, c, rows(half), cols(p)], acc.at[:, :, :, rows(half), cols(p)],
-                                     p_sem.at[k])
+    early = g_ref.shape[1]
+
+    def a_copy(i):
+        return pltpu.make_async_copy(ws1_hbm.at[:, pl.ds(early + i * CH, CH)], a_v.at[i], a_sem.at[i])
+
+    def b_copy(i):
+        return pltpu.make_async_copy(ws3_hbm.at[:, pl.ds(early + i * CH, CH)], b_v.at[i], b_sem.at[i])
 
     def swap(k):
         p, half = streams[k]
         return pltpu.make_async_remote_copy(
-            p_hbm.at[:, :, :, 1 - c, rows(half), cols(p)], r0.at[:, :, :, rows(half), cols(p)], s0.at[k], q0.at[k],
+            p_ref.at[:, :, :, 1 - c, rows(half), cols(p)], r0.at[:, :, :, rows(half), cols(p)], s0.at[k], q0.at[k],
             device_id=_dev(z, y, x, 1 - c), device_id_type=MESH)
 
     def region(ref, p, half, step, mine):
@@ -548,8 +550,9 @@
             region(acc, p, half, step, False), landing(p, half, step), send.at[k], recv.at[k],
             device_id=_dev(*o, c), device_id_type=MESH)
 
-    for k in range(NS):
-        load(k).start()
+    for i in range(LATE):
+        a_copy(i).start()
+        b_copy(i).start()
     barrier = pltpu.get_barrier_semaphore()
     pl.semaphore_signal(barrier, inc=1, device_id=_dev(z, y, x, 1 - c), device_id_type=MESH)
     for d in (1, 2, 4):
@@ -563,24 +566,32 @@
     def shared(i):
         w_copy(i).wait()
         cs = slice(i * wn, (i + 1) * wn)
-        sh[:, cs] = jnp.dot(g_ref[...], w_v[i], preferred_element_type=F32) + h_ref[:, cs].astype(F32)
+        s = jnp.dot(g_ref[...], w_v[i, 0:early], preferred_element_type=F32)
+        s += jnp.dot(late[...], w_v[i, early:], preferred_element_type=F32)
+        sh[:, cs] = s + h_ref[:, cs].astype(F32)
+
+    def up(i):
+        a_copy(i).wait()
+        b_copy(i).wait()
+        late[:, i * CH:(i + 1) * CH] = _silu_mul(jnp.dot(u_ref[...], a_v[i], preferred_element_type=F32),
+                                                 jnp.dot(u_ref[...], b_v[i], preferred_element_type=F32))
 
     for k in range(NS):
         p, half = streams[k]
-        load(k).wait()
         swap(k).wait_recv()
         rs, cs = slice(half * ROWS, half * ROWS + ROWS), slice(COLS[p][0], COLS[p][0] + COLS[p][1])
-        acc[:, :, :, rs, cs] += r0[:, :, :, rs, cs]
+        acc[:, :, :, rs, cs] = p_ref[:, :, :, c, rs, cs] + r0[:, :, :, rs, cs]
         hop(k, 1).start()
-    shared(0)
+    for i in range(LATE):
+        up(i)
     for k in range(NS):
         p, half = streams[k]
         hop(k, 1).wait_recv()
         v = region(acc, p, half, 1, True)
         v[...] += landing(p, half, 1)[...]
         hop(k, 2).start()
-    shared(1)
-    shared(2)
+    for i in range(3):
+        shared(i)
     for k in range(NS):
         p, half = streams[k]
         hop(k, 2).wait_recv()
@@ -602,7 +613,7 @@
             hop(k, step).wait_send()
 
 
-def _combine(part, g, h, ws2):
+def _combine(part, g, h, u, ws1, ws3, ws2):
     b, d = h.shape
     fs = ws2.shape[0]
     nw = 8
@@ -610,7 +621,7 @@
     return pl.pallas_call(
         _combine_kernel,
         out_shape=jax.ShapeDtypeStruct((b, d), BF16),
-        in_specs=[HBM, VMEM, VMEM, HBM],
+        in_specs=[VMEM, VMEM, VMEM, VMEM, HBM, HBM, HBM],
         out_specs=VMEM,
         scratch_shapes=[
             pltpu.VMEM((2, 2, 2, b, d), F32),
@@ -619,21 +630,24 @@
             pltpu.VMEM((2, b, d), F32),
             pltpu.VMEM((b, d), F32),
             pltpu.VMEM((nw, fs, d // nw), BF16),
+            pltpu.VMEM((LATE, d, CH), BF16),
+            pltpu.VMEM((LATE, d, CH), BF16),
+            pltpu.VMEM((b, LATE * CH), BF16),
             pltpu.VMEM((b, d), F32),
-            DMA((nw,)), DMA((NS,)),
+            DMA((nw,)), DMA((LATE,)), DMA((LATE,)),
             DMA((NS,)), DMA((NS,)), DMA((NS,)), DMA((NS,)), DMA((NS,)), DMA((NS,)), DMA((NS,)), DMA((NS,)),
         ],
-        compiler_params=pltpu.CompilerParams(vmem_limit_bytes=62 * 2 ** 20, collective_id=1, has_side_effects=True),
+        compiler_params=pltpu.CompilerParams(vmem_limit_bytes=52 * 2 ** 20, collective_id=1, has_side_effects=True),
         name="combine",
-    )(part, g, h, ws2)
+    )(part, g, h, u, ws1, ws3, ws2)
 
 
 def solution(mesh):
     def body(x, kv_k, kv_v, lens, idx, gates, ln1, wq, wo, ln2, ws1, ws3, ws2, w1, w3, w2):
         b, d = x.shape
-        h, hall, g, key, gsel, krow, cnt = _front(x, kv_k, kv_v, lens, idx, gates, ln1, ln2, wq, wo, ws1, ws3)
-        part = _experts(hall.reshape(16 * b, d), ln2, key, gsel, krow, cnt, w1, w3, w2, b)
-        return _combine(part, g, h, ws2)
+        h, u, uall, g, key, gsel, krow, cnt = _front(x, kv_k, kv_v, lens, idx, gates, ln1, ln2, wq, wo, ws1, ws3)
+        part = _experts(uall.reshape(16 * b, d), key, gsel, krow, cnt, w1, w3, w2, b)
+        return _combine(part, g, h, u, ws1, ws3, ws2)
 
     rows = P(GRP)
     rep = P()

time: 110 us -> 98 us (0.89)
  Pallas kernels: 108 us -> 97.1 us
    pallas_call x1, Pallas kernels: 32.8 us -> 26.4 us  [_experts(): pl.pallas_call(functools.partial(_expert_kernel, big), out_shape=jax.Shap...]
    pallas_call x1, Pallas kernels: 38.1 us -> 34.5 us  [_combine(): pl.pallas_call(_combine_kernel, out_shape=jax.ShapeDtypeStruct((b, d), BF...]
where the time goes in v3:
time: 98 us; the launch traced here: 97.8 us
  Pallas kernels  97.1 us (99%)
    pallas_call x1, Pallas kernels, _front(): pl.pallas_call(functools.partial(_front_kernel, b - b // 8), out_shape=[j...  36.1 us
    pallas_call x1, Pallas kernels, _combine(): pl.pallas_call(_combine_kernel, out_shape=jax.ShapeDtypeStruct((b, d), BF...  34.5 us
    pallas_call x1, Pallas kernels, _experts(): pl.pallas_call(functools.partial(_expert_kernel, big), out_shape=jax.Shap...  26.4 us

profile of v3, /device:TPU:0, one launch (start us, length us, event | category | flops | bytes accessed | tf_op | source)
XLA Modules:
  0.0 97.8 jit_solution(1126967629272538649)
XLA Ops:
  0.0 36.1 %front.1 = (bf16[32,2048]{1,0:T(8,128)(2,1)}, bf16[32,2048]{1,0:T(8,128)(2,1)}, bf16[16,32,2048]{2,1,0:T(8,128)(2,1)}, bf16[32,4096]{1,0:T(8,128)(2,1)}, f32[512...) custom-call(bf16[32,2048]{1,0:T(8,128)(2,1)} %x_ref.1, bf16[16,128]{1,0:T(8,128)(2,1)} %bitcast.12, ...), custom_call_target="tpu_custom_call" | custom-call | tf_op jit(solution)/shard_map/front/pallas_call | solution.py:300
  36.1 0.0 copy-start
  36.2 0.0 copy-start.1
  36.2 0.0 copy-start.2
  36.2 26.4 %experts.1 = f32[512,2048]{1,0:T(8,128)} custom-call(bf16[512,2048]{1,0:T(8,128)(2,1)} %bitcast.11, f32[512,128]{1,0:T(8,128)} %get-tuple-element.14.key_ref, f32[512,128]{1,0:T(8,128)} %get-tuple-element.15.gsel_ref, f32[8,512]{1,0:T(8,128)} %get-tuple-element.16.krow, s32[2,128]{1,0:T(2,128)} %get-tuple-element.17.cnt, bf16[4,2048,1408]{2,1,0:T(8,128)(2,1)} %w1_hbm.1, ...), custom_call_target="tpu_custom_call" | custom-call | tf_op jit(solution)/shard_map/experts/pallas_call | solution.py:469
  62.6 0.0 copy-done
  62.6 0.0 copy-done.1
  62.6 0.0 copy-done.2
  62.6 34.5 %combine.1 = bf16[32,2048]{1,0:T(8,128)(2,1)S(1)} custom-call(f32[2,2,2,2,32,2048]{5,4,3,2,1,0:T(8,128)} %bitcast.8, bf16[32,4096]{1,0:T(8,128)(2,1)S(1)} %copy-done, bf16[32,2048]{1,0:T(8,128)(2,1)S(1)} %copy-done.1, bf16[32,2048]{1,0:T(8,128)(2,1)S(1)} %copy-done.2, bf16[2048,5632]{1,0:T(8,128)(2,1)} %ws1_hbm.3, bf16[2048,5632]{1,0:T(8,128)(2,1)} %ws3_hbm.3, ...), custom_call_target="tpu_custom_call" | custom-call | tf_op jit(solution)/shard_map/combine/pallas_call | solution.py:621
  97.1 0.7 copy.18
Async XLA Ops:
  36.1 26.4 %copy-start = (bf16[32,4096]{1,0:T(8,128)(2,1)S(1)}, bf16[32,4096]{1,0:T(8,128)(2,1)}, u32[]{:S(2)}) copy-start(bf16[32,4096]{1,0:T(8,128)(2,1)} %get-tuple-element.18.g_ref) | copy-start | bytes 786436
  36.2 26.4 %copy-start.1 = (bf16[32,2048]{1,0:T(8,128)(2,1)S(1)}, bf16[32,2048]{1,0:T(8,128)(2,1)}, u32[]{:S(2)}) copy-start(bf16[32,2048]{1,0:T(8,128)(2,1)} %get-tuple-element.19.h_ref) | copy-start | bytes 393220
  36.2 26.4 %copy-start.2 = (bf16[32,2048]{1,0:T(8,128)(2,1)S(1)}, bf16[32,2048]{1,0:T(8,128)(2,1)}, u32[]{:S(2)}) copy-start(bf16[32,2048]{1,0:T(8,128)(2,1)} %get-tuple-element.20.u_ref) | copy-start | bytes 393220

commit v4 on v3

--- a/solution.py
+++ b/solution.py
@@ -160,14 +160,17 @@
 
     no = d // CH
 
-    def send(o, i):
-        dev = _dev(*_offset((z, y, x), o), c) if o else _dev(z, y, x, 1 - c)
-        return pltpu.make_async_remote_copy(h_ref.at[:, cols(i)], ha.at[me, :, cols(i)], us_send.at[o, i],
-                                            us_recv.at[o, i], device_id=dev, device_id_type=MESH)
-
     def source(o, core):
         oz, oy, ox = _offset((z, y, x), o)
         return ((oz * 2 + oy) * 2 + ox) * 2 + core
+
+    def send(o, i):
+        via = {3: (1, 2), 6: (2, 4), 5: (4, 1), 7: ((3, 4), (6, 1), (5, 2))[i % 3]}
+        held, to = via.get(o, (0, o))
+        src = ha.at[source(held, c), :, cols(i)] if held else h_ref.at[:, cols(i)]
+        dev = _dev(*_offset((z, y, x), to), c) if o else _dev(z, y, x, 1 - c)
+        return pltpu.make_async_remote_copy(src, ha.at[source(held, c), :, cols(i)], us_send.at[o, i],
+                                            us_recv.at[o, i], device_id=dev, device_id_type=MESH)
 
     def forward(o, i):
         at = ha.at[source(o, c), :, cols(i)]
@@ -178,7 +181,16 @@
         src = source(o, core)
         return pltpu.make_async_copy(ua.at[src], uall_hbm.at[src], out_sem.at[2 * o + (0 if core is c else 1)])
 
-    order = (7, 6, 5, 3, 4, 2, 1, 0)
+    def arrived(level, i):
+        for o in ((1, 2, 4), (3, 6, 5), (7,))[level]:
+            send(o, i).wait_recv()
+            if level == 0:
+                send({1: 3, 2: 6, 4: 5}[o], i).start()
+            if level == 1 and o == (3, 6, 5)[i % 3]:
+                send(7, i).start()
+            forward(o, i).start()
+
+    order = (1, 2, 4, 3, 6, 5, 7)
     for i in range(no):
         acc = x_ref[:, cols(i)].astype(F32)
         attn = jnp.zeros((b, CH), F32)
@@ -186,12 +198,12 @@
             o_copy(i * 2 + t).wait()
             attn += jnp.dot(ob[:, t * d:(t + 1) * d], ring[lax.rem(nq + i * 2 + t, RING)], preferred_element_type=F32)
         h_ref[:, cols(i)] = (acc + attn).astype(BF16)
-        for cp in w_copies(ahead + i):
+        for cp in w_copies(ahead + i) if ahead + i < nw else ():
             cp.start()
-        for o in order:
+        for o in (1, 2, 4, 0):
             send(o, i).start()
 
-    ahead += no
+    ahead = min(ahead + no, nw)
     ln2 = _row(ln2_ref)
     us[...] = _rms(h_ref[...].astype(F32), ln2)
 
@@ -206,6 +218,8 @@
 
     ua[me] = us[...]
     shared(0)
+    arrived(0, 0)
+    arrived(0, 1)
 
     n = 0
     while ahead < nw:
@@ -247,31 +261,31 @@
         krow_ref[:, sl] = key.T[0:8]
         cnt_ref[g:g + 1, :] = jnp.sum(keep, axis=0, keepdims=True).astype(jnp.int32)
 
-    for i in range(n if n else 1, nw):
-        shared(i)
-        at = {1: 0, 3: 1, 5: 2, 7: 3}.get(i)
-        if at is not None:
-            for o in order[:-1]:
-                send(o, at).wait_recv()
-                forward(o, at).start()
-
     def normalise(o, core):
         src = source(o, core)
         ua[src] = _rms(ha[src].astype(F32), ln2)
 
-    for o in order[:-1]:
-        normalise(o, c)
-    for o in range(8):
-        store(o, c).start()
-    for t in range(no):
-        send(0, t).wait_recv()
-    for o in order[:-1]:
-        for t in range(no):
-            forward(o, t).wait_recv()
-    for o in range(8):
-        normalise(o, 1 - c)
-    for o in range(8):
-        store(o, 1 - c).start()
+    for i in range(n if n else 1, nw):
+        shared(i)
+        for step in {1: ((0, 2), (1, 0)), 2: ((0, 3), (1, 1)), 3: ((1, 2), (2, 0)), 4: ((1, 3), (2, 1)),
+                     5: ((2, 2), (2, 3))}.get(i, ()):
+            arrived(*step)
+        if i == nw - 3:
+            for o in order:
+                normalise(o, c)
+            for o in range(8):
+                store(o, c).start()
+        if i == nw - 2:
+            for t in range(no):
+                send(0, t).wait_recv()
+            for o in order:
+                for t in range(no):
+                    forward(o, t).wait_recv()
+            for o in range(8):
+                normalise(o, 1 - c)
+            for o in range(8):
+                store(o, 1 - c).start()
+
     for o in range(8):
         for t in range(no):
             send(o, t).wait_send()
@@ -328,8 +342,8 @@
 SMALL = 32
 
 
-def _expert_kernel(big, u_hbm, key_ref, gsel_ref, krow, cnt, w1_hbm, w3_hbm, w2_hbm, p_ref,
-                   u_v, xs, zs, w1_v, w3_v, w2_v, mid, order, u_sem, w_sem):
+def _expert_kernel(big, u_hbm, key_hbm, gsel_hbm, krow, cnt, w1_hbm, w3_hbm, w2_hbm, p_ref,
+                   u_v, xs, zs, w1_v, w3_v, w2_v, mid, key_ref, gsel_ref, order, u_sem, k_sem, w_sem):
     t, d = u_v.shape
     ng = t // GROUP
     u_copy = pltpu.make_async_copy(u_hbm, u_v, u_sem)
@@ -360,6 +374,11 @@
         w1_copy(i).start()
         w3_copy(i).start()
         w2_copy(i).start()
+        if i == 0:
+            k_copies = (pltpu.make_async_copy(key_hbm, key_ref, k_sem.at[0]),
+                        pltpu.make_async_copy(gsel_hbm, gsel_ref, k_sem.at[1]))
+            for cp in k_copies:
+                cp.start()
     p_ref[...] = jnp.zeros_like(p_ref)
     u_copy.wait()
     lane = lax.broadcasted_iota(jnp.int32, (GROUP, 128), 1)
@@ -444,6 +463,11 @@
 
         w2_copy(i).wait()
 
+        @pl.when(i == 0)
+        def _():
+            for cp in k_copies:
+                cp.wait()
+
         @pl.when(few)
         def _():
             out = down(mid[both, :], s)
@@ -469,7 +493,7 @@
     return pl.pallas_call(
         functools.partial(_expert_kernel, big),
         out_shape=jax.ShapeDtypeStruct((t, d), F32),
-        in_specs=[HBM, VMEM, VMEM, VMEM, SMEM, HBM, HBM, HBM],
+        in_specs=[HBM, HBM, HBM, VMEM, SMEM, HBM, HBM, HBM],
         out_specs=VMEM,
         scratch_shapes=[
             pltpu.VMEM((t, d), BF16),
@@ -479,8 +503,10 @@
             pltpu.VMEM((2, d, f), BF16),
             pltpu.VMEM((2, f, d), BF16),
             pltpu.VMEM((slots, f), BF16),
+            pltpu.VMEM((t, 128), F32),
+            pltpu.VMEM((t, 128), F32),
             pltpu.SMEM((EDEV,), jnp.int32),
-            DMA(()), DMA((2, 3)),
+            DMA(()), DMA((2,)), DMA((2, 3)),
         ],
         compiler_params=pltpu.CompilerParams(vmem_limit_bytes=55 * 2 ** 20),
         name="experts",
@@ -492,8 +518,8 @@
 NS = 3 * PARTS
 
 
-def _combine_kernel(p_ref, g_ref, h_ref, u_ref, ws1_hbm, ws3_hbm, w_hbm, y_ref,
-                    acc, r0, r1, r2, r3, w_v, a_v, b_v, late, sh, w_sem, a_sem, b_sem,
+def _combine_kernel(p_hbm, g_ref, h_ref, u_ref, ws1_hbm, ws3_hbm, w_hbm, y_ref,
+                    acc, r0, r1, r2, r3, w_v, a_v, b_v, late, sh, w_sem, a_sem, b_sem, p_sem,
                     s0, q0, s1, q1, s2, q2, s3, q3):
     z, y, x, c = _place()
     nw, _, wn = w_v.shape
@@ -518,10 +544,15 @@
     def b_copy(i):
         return pltpu.make_async_copy(ws3_hbm.at[:, pl.ds(early + i * CH, CH)], b_v.at[i], b_sem.at[i])
 
+    def load(k):
+        p, half = streams[k]
+        return pltpu.make_async_copy(p_hbm.at[:, :, :, c, rows(half), cols(p)], acc.at[:, :, :, rows(half), cols(p)],
+                                     p_sem.at[k])
+
     def swap(k):
         p, half = streams[k]
         return pltpu.make_async_remote_copy(
-            p_ref.at[:, :, :, 1 - c, rows(half), cols(p)], r0.at[:, :, :, rows(half), cols(p)], s0.at[k], q0.at[k],
+            p_hbm.at[:, :, :, 1 - c, rows(half), cols(p)], r0.at[:, :, :, rows(half), cols(p)], s0.at[k], q0.at[k],
             device_id=_dev(z, y, x, 1 - c), device_id_type=MESH)
 
     def region(ref, p, half, step, mine):
@@ -550,6 +581,8 @@
             region(acc, p, half, step, False), landing(p, half, step), send.at[k], recv.at[k],
             device_id=_dev(*o, c), device_id_type=MESH)
 
+    for k in range(NS):
+        load(k).start()
     for i in range(LATE):
         a_copy(i).start()
         b_copy(i).start()
@@ -578,35 +611,36 @@
 
     for k in range(NS):
         p, half = streams[k]
+        load(k).wait()
         swap(k).wait_recv()
         rs, cs = slice(half * ROWS, half * ROWS + ROWS), slice(COLS[p][0], COLS[p][0] + COLS[p][1])
-        acc[:, :, :, rs, cs] = p_ref[:, :, :, c, rs, cs] + r0[:, :, :, rs, cs]
+        acc[:, :, :, rs, cs] += r0[:, :, :, rs, cs]
         hop(k, 1).start()
     for i in range(LATE):
         up(i)
+
+    def add(k, step):
+        p, half = streams[k]
+        hop(k, step).wait_recv()
+        v = region(acc, p, half, step, True)
+        if step < 3:
+            v[...] += landing(p, half, step)[...]
+            hop(k, step + 1).start()
+        else:
+            tot = v[...] + landing(p, half, 3)[...]
+            rs, cs = slice(half * ROWS, half * ROWS + ROWS), slice(COLS[p][0], COLS[p][0] + COLS[p][1])
+            y_ref[rs, cs] = (sh[rs, cs] + tot).astype(BF16)
+
     for k in range(NS):
-        p, half = streams[k]
-        hop(k, 1).wait_recv()
-        v = region(acc, p, half, 1, True)
-        v[...] += landing(p, half, 1)[...]
-        hop(k, 2).start()
-    for i in range(3):
-        shared(i)
+        add(k, 1)
+        if k % 3 == 2:
+            shared(k // 3)
+        if k >= 6:
+            add(k - 6, 2)
+    for k in range(6, NS):
+        add(k, 2)
     for k in range(NS):
-        p, half = streams[k]
-        hop(k, 2).wait_recv()
-        v = region(acc, p, half, 2, True)
-        v[...] += landing(p, half, 2)[...]
-        hop(k, 3).start()
-    for i in range(3, nw):
-        shared(i)
-    for k in range(NS):
-        p, half = streams[k]
-        hop(k, 3).wait_recv()
-        v = region(acc, p, half, 3, True)
-        tot = v[...] + landing(p, half, 3)[...]
-        rs, cs = slice(half * ROWS, half * ROWS + ROWS), slice(COLS[p][0], COLS[p][0] + COLS[p][1])
-        y_ref[rs, cs] = (sh[rs, cs] + tot).astype(BF16)
+        add(k, 3)
     for k in range(NS):
         swap(k).wait_send()
         for step in (1, 2, 3):
@@ -616,12 +650,12 @@
 def _combine(part, g, h, u, ws1, ws3, ws2):
     b, d = h.shape
     fs = ws2.shape[0]
-    nw = 8
+    nw = 4
     part = part.reshape(2, 2, 2, 2, b, d)
     return pl.pallas_call(
         _combine_kernel,
         out_shape=jax.ShapeDtypeStruct((b, d), BF16),
-        in_specs=[VMEM, VMEM, VMEM, VMEM, HBM, HBM, HBM],
+        in_specs=[HBM, VMEM, VMEM, VMEM, HBM, HBM, HBM],
         out_specs=VMEM,
         scratch_shapes=[
             pltpu.VMEM((2, 2, 2, b, d), F32),
@@ -634,10 +668,10 @@
             pltpu.VMEM((LATE, d, CH), BF16),
             pltpu.VMEM((b, LATE * CH), BF16),
             pltpu.VMEM((b, d), F32),
-            DMA((nw,)), DMA((LATE,)), DMA((LATE,)),
+            DMA((nw,)), DMA((LATE,)), DMA((LATE,)), DMA((NS,)),
             DMA((NS,)), DMA((NS,)), DMA((NS,)), DMA((NS,)), DMA((NS,)), DMA((NS,)), DMA((NS,)), DMA((NS,)),
         ],
-        compiler_params=pltpu.CompilerParams(vmem_limit_bytes=52 * 2 ** 20, collective_id=1, has_side_effects=True),
+        compiler_params=pltpu.CompilerParams(vmem_limit_bytes=50 * 2 ** 20, collective_id=1, has_side_effects=True),
         name="combine",
     )(part, g, h, u, ws1, ws3, ws2)
 

time: 98 us -> 96.9 us (0.989)
  Pallas kernels: 97.1 us -> 96 us
    pallas_call x1, Pallas kernels: 34.5 us -> 30.8 us  [_combine(): pl.pallas_call(_combine_kernel, out_shape=jax.ShapeDtypeStruct((b, d), BF...]
    pallas_call x1, Pallas kernels: 26.4 us -> 27.8 us  [_experts(): pl.pallas_call(functools.partial(_expert_kernel, big), out_shape=jax.Shap...]
    pallas_call x1, Pallas kernels: 36.1 us -> 37.4 us  [_front(): pl.pallas_call(functools.partial(_front_kernel, b - b // 8), out_shape=[j...]
where the time goes in v4:
time: 96.9 us; the launch traced here: 96.7 us
  Pallas kernels  96 us (99%)
    pallas_call x1, Pallas kernels, _front(): pl.pallas_call(functools.partial(_front_kernel, b - b // 8), out_shape=[j...  37.4 us
    pallas_call x1, Pallas kernels, _combine(): pl.pallas_call(_combine_kernel, out_shape=jax.ShapeDtypeStruct((b, d), BF...  30.8 us
    pallas_call x1, Pallas kernels, _experts(): pl.pallas_call(functools.partial(_expert_kernel, big), out_shape=jax.Shap...  27.8 us

profile of v4, /device:TPU:0, one launch (start us, length us, event | category | flops | bytes accessed | tf_op | source)
XLA Modules:
  0.0 96.7 jit_solution(9717675260587521988)
XLA Ops:
  0.0 37.4 %front.1 = (bf16[32,2048]{1,0:T(8,128)(2,1)}, bf16[32,2048]{1,0:T(8,128)(2,1)}, bf16[16,32,2048]{2,1,0:T(8,128)(2,1)}, bf16[32,4096]{1,0:T(8,128)(2,1)}, f32[512...) custom-call(bf16[32,2048]{1,0:T(8,128)(2,1)} %x_ref.1, bf16[16,128]{1,0:T(8,128)(2,1)} %bitcast.12, ...), custom_call_target="tpu_custom_call" | custom-call | tf_op jit(solution)/shard_map/front/pallas_call | solution.py:314
  37.4 0.0 copy-start
  37.4 0.0 copy-start.1
  37.4 0.0 copy-start.2
  37.4 27.8 %experts.1 = f32[512,2048]{1,0:T(8,128)} custom-call(bf16[512,2048]{1,0:T(8,128)(2,1)} %bitcast.11, f32[512,128]{1,0:T(8,128)} %get-tuple-element.14.key_hbm, f32[512,128]{1,0:T(8,128)} %get-tuple-element.15.gsel_hbm, f32[8,512]{1,0:T(8,128)} %get-tuple-element.16.krow, s32[2,128]{1,0:T(2,128)} %get-tuple-element.17.cnt, bf16[4,2048,1408]{2,1,0:T(8,128)(2,1)} %w1_hbm.1, ...), custom_call_target="tpu_custom_call" | custom-call | tf_op jit(solution)/shard_map/experts/pallas_call | solution.py:493
  65.2 0.0 copy-done
  65.2 0.0 copy-done.1
  65.3 0.0 copy-done.2
  65.3 30.8 %combine.1 = bf16[32,2048]{1,0:T(8,128)(2,1)S(1)} custom-call(f32[2,2,2,2,32,2048]{5,4,3,2,1,0:T(8,128)} %bitcast.8, bf16[32,4096]{1,0:T(8,128)(2,1)S(1)} %copy-done, bf16[32,2048]{1,0:T(8,128)(2,1)S(1)} %copy-done.1, bf16[32,2048]{1,0:T(8,128)(2,1)S(1)} %copy-done.2, bf16[2048,5632]{1,0:T(8,128)(2,1)} %ws1_hbm.3, bf16[2048,5632]{1,0:T(8,128)(2,1)} %ws3_hbm.3, ...), custom_call_target="tpu_custom_call" | custom-call | tf_op jit(solution)/shard_map/combine/pallas_call | solution.py:655
  96.1 0.7 copy.18
Async XLA Ops:
  37.4 27.8 %copy-start = (bf16[32,4096]{1,0:T(8,128)(2,1)S(1)}, bf16[32,4096]{1,0:T(8,128)(2,1)}, u32[]{:S(2)}) copy-start(bf16[32,4096]{1,0:T(8,128)(2,1)} %get-tuple-element.18.g_ref) | copy-start | bytes 786436
  37.4 27.8 %copy-start.1 = (bf16[32,2048]{1,0:T(8,128)(2,1)S(1)}, bf16[32,2048]{1,0:T(8,128)(2,1)}, u32[]{:S(2)}) copy-start(bf16[32,2048]{1,0:T(8,128)(2,1)} %get-tuple-element.19.h_ref) | copy-start | bytes 393220
  37.4 27.8 %copy-start.2 = (bf16[32,2048]{1,0:T(8,128)(2,1)S(1)}, bf16[32,2048]{1,0:T(8,128)(2,1)}, u32[]{:S(2)}) copy-start(bf16[32,2048]{1,0:T(8,128)(2,1)} %get-tuple-element.20.u_ref) | copy-start | bytes 393220

commit v5 on v4

--- a/solution.py
+++ b/solution.py
@@ -342,8 +342,8 @@
 SMALL = 32
 
 
-def _expert_kernel(big, u_hbm, key_hbm, gsel_hbm, krow, cnt, w1_hbm, w3_hbm, w2_hbm, p_ref,
-                   u_v, xs, zs, w1_v, w3_v, w2_v, mid, key_ref, gsel_ref, order, u_sem, k_sem, w_sem):
+def _expert_kernel(big, u_hbm, key_hbm, gsel_hbm, krow, cnt, w1_hbm, w3_hbm, w2_hbm, p_hbm, p_ref,
+                   u_v, xs, zs, w1_v, w3_v, w2_v, mid, key_ref, gsel_ref, order, u_sem, k_sem, p_sem, w_sem):
     t, d = u_v.shape
     ng = t // GROUP
     u_copy = pltpu.make_async_copy(u_hbm, u_v, u_sem)
@@ -403,8 +403,13 @@
             back = jnp.dot(sel, out[:, cs], preferred_element_type=F32)
             p_ref[tl, cs] += back * gt
 
-    def slots(g):
-        return pl.ds(pl.multiple_of(g * big, 16), big)
+    def p_copy(g):
+        return pltpu.make_async_copy(p_ref.at[tokens(g)], p_hbm.at[tokens(g)], p_sem.at[g])
+
+    def done(i, g):
+        @pl.when(i == EDEV - 1)
+        def _():
+            p_copy(g).start()
 
     def down(g, s):
         return jnp.dot(g, w2_v[s], preferred_element_type=F32).astype(BF16)
@@ -424,9 +429,8 @@
 
         @pl.when(many)
         def _():
-            @pl.loop(0, ng)
-            def _(g):
-                xs[slots(g), :] = pick(e, g, big)
+            for g in range(ng):
+                xs[g * big:(g + 1) * big, :] = pick(e, g, big)
 
         w1_copy(i).wait()
 
@@ -436,9 +440,7 @@
 
         @pl.when(many)
         def _():
-            @pl.loop(0, ng)
-            def _(g):
-                zs[slots(g), :] = jnp.dot(xs[slots(g), :], w1_v[s], preferred_element_type=F32)
+            zs[...] = jnp.dot(xs[...], w1_v[s], preferred_element_type=F32)
 
         @pl.when(i + 2 < EDEV)
         def _():
@@ -452,10 +454,7 @@
 
         @pl.when(many)
         def _():
-            @pl.loop(0, ng)
-            def _(g):
-                mid[slots(g), :] = _silu_mul(
-                    zs[slots(g), :], jnp.dot(xs[slots(g), :], w3_v[s], preferred_element_type=F32))
+            mid[...] = _silu_mul(zs[...], jnp.dot(xs[...], w3_v[s], preferred_element_type=F32))
 
         @pl.when(i + 2 < EDEV)
         def _():
@@ -473,16 +472,26 @@
             out = down(mid[both, :], s)
             for g in range(ng):
                 put(e, g, SMALL, out[g * SMALL:(g + 1) * SMALL])
+                done(i, g)
 
         @pl.when(many)
         def _():
-            @pl.loop(0, ng)
-            def _(g):
-                put(e, g, big, down(mid[slots(g), :], s))
+            out = down(mid[...], s)
+            for g in range(ng):
+                put(e, g, big, out[g * big:(g + 1) * big])
+                done(i, g)
+
+        @pl.when(most == 0)
+        def _():
+            for g in range(ng):
+                done(i, g)
 
         @pl.when(i + 2 < EDEV)
         def _():
             w2_copy(i + 2).start()
+
+    for g in range(ng):
+        p_copy(g).wait()
 
 
 def _experts(u, key, gsel, krow, cnt, w1, w3, w2, blk):
@@ -494,8 +503,9 @@
         functools.partial(_expert_kernel, big),
         out_shape=jax.ShapeDtypeStruct((t, d), F32),
         in_specs=[HBM, HBM, HBM, VMEM, SMEM, HBM, HBM, HBM],
-        out_specs=VMEM,
+        out_specs=HBM,
         scratch_shapes=[
+            pltpu.VMEM((t, d), F32),
             pltpu.VMEM((t, d), BF16),
             pltpu.VMEM((slots, d), BF16),
             pltpu.VMEM((slots, f), F32),
@@ -506,7 +516,7 @@
             pltpu.VMEM((t, 128), F32),
             pltpu.VMEM((t, 128), F32),
             pltpu.SMEM((EDEV,), jnp.int32),
-            DMA(()), DMA((2,)), DMA((2, 3)),
+            DMA(()), DMA((2,)), DMA((t // GROUP,)), DMA((2, 3)),
         ],
         compiler_params=pltpu.CompilerParams(vmem_limit_bytes=55 * 2 ** 20),
         name="experts",

time: 96.9 us -> 95.7 us (0.988)
  Pallas kernels: 96 us -> 94.8 us
where the time goes in v5:
time: 95.7 us; the launch traced here: 95.5 us
  Pallas kernels  94.8 us (99%)
    pallas_call x1, Pallas kernels, _front(): pl.pallas_call(functools.partial(_front_kernel, b - b // 8), out_shape=[j...  37.4 us
    pallas_call x1, Pallas kernels, _combine(): pl.pallas_call(_combine_kernel, out_shape=jax.ShapeDtypeStruct((b, d), BF...  30 us
    pallas_call x1, Pallas kernels, _experts(): pl.pallas_call(functools.partial(_expert_kernel, big), out_shape=jax.Shap...  27.4 us

profile of v5, /device:TPU:0, one launch (start us, length us, event | category | flops | bytes accessed | tf_op | source)
XLA Modules:
  0.0 95.5 jit_solution(12797004729602938161)
XLA Ops:
  0.0 37.4 %front.1 = (bf16[32,2048]{1,0:T(8,128)(2,1)}, bf16[32,2048]{1,0:T(8,128)(2,1)}, bf16[16,32,2048]{2,1,0:T(8,128)(2,1)}, bf16[32,4096]{1,0:T(8,128)(2,1)}, f32[512...) custom-call(bf16[32,2048]{1,0:T(8,128)(2,1)} %x_ref.1, bf16[16,128]{1,0:T(8,128)(2,1)} %bitcast.12, ...), custom_call_target="tpu_custom_call" | custom-call | tf_op jit(solution)/shard_map/front/pallas_call | solution.py:314
  37.4 0.0 copy-start
  37.4 0.0 copy-start.1
  37.4 0.0 copy-start.2
  37.4 27.4 %experts.1 = f32[512,2048]{1,0:T(8,128)} custom-call(bf16[512,2048]{1,0:T(8,128)(2,1)} %bitcast.11, f32[512,128]{1,0:T(8,128)} %get-tuple-element.14.key_hbm, f32[512,128]{1,0:T(8,128)} %get-tuple-element.15.gsel_hbm, f32[8,512]{1,0:T(8,128)} %get-tuple-element.16.krow, s32[2,128]{1,0:T(2,128)} %get-tuple-element.17.cnt, bf16[4,2048,1408]{2,1,0:T(8,128)(2,1)} %w1_hbm.1, ...), custom_call_target="tpu_custom_call" | custom-call | tf_op jit(solution)/shard_map/experts/pallas_call | solution.py:502
  64.9 0.0 copy-done
  64.9 0.0 copy-done.1
  64.9 0.0 copy-done.2
  64.9 30.0 %combine.1 = bf16[32,2048]{1,0:T(8,128)(2,1)S(1)} custom-call(f32[2,2,2,2,32,2048]{5,4,3,2,1,0:T(8,128)} %bitcast.8, bf16[32,4096]{1,0:T(8,128)(2,1)S(1)} %copy-done, bf16[32,2048]{1,0:T(8,128)(2,1)S(1)} %copy-done.1, bf16[32,2048]{1,0:T(8,128)(2,1)S(1)} %copy-done.2, bf16[2048,5632]{1,0:T(8,128)(2,1)} %ws1_hbm.3, bf16[2048,5632]{1,0:T(8,128)(2,1)} %ws3_hbm.3, ...), custom_call_target="tpu_custom_call" | custom-call | tf_op jit(solution)/shard_map/combine/pallas_call | solution.py:665
  94.9 0.7 copy.18
Async XLA Ops:
  37.4 27.5 %copy-start = (bf16[32,4096]{1,0:T(8,128)(2,1)S(1)}, bf16[32,4096]{1,0:T(8,128)(2,1)}, u32[]{:S(2)}) copy-start(bf16[32,4096]{1,0:T(8,128)(2,1)} %get-tuple-element.18.g_ref) | copy-start | bytes 786436
  37.4 27.5 %copy-start.1 = (bf16[32,2048]{1,0:T(8,128)(2,1)S(1)}, bf16[32,2048]{1,0:T(8,128)(2,1)}, u32[]{:S(2)}) copy-start(bf16[32,2048]{1,0:T(8,128)(2,1)} %get-tuple-element.19.h_ref) | copy-start | bytes 393220
  37.4 27.5 %copy-start.2 = (bf16[32,2048]{1,0:T(8,128)(2,1)S(1)}, bf16[32,2048]{1,0:T(8,128)(2,1)}, u32[]{:S(2)}) copy-start(bf16[32,2048]{1,0:T(8,128)(2,1)} %get-tuple-element.20.u_ref) | copy-start | bytes 393220
